TPU v7x, 32 devices: a whole 2x2x4 slice. The times are simulated.
32 devices in a mesh: fsdp: 8 (over z, y), dp: 4 (over x, core).
Axes of the slice: x: 2, y: 2, z: 4, core: 2. Of those that a mesh axis runs over, the one named last changes fastest.
Arguments:
- tokens: bfloat16 [32, 128, 3584], P(('fsdp', 'dp')), may hold values from -6 to 6
- lengths: int32 [32], P(('fsdp', 'dp')), may hold values from 32 to 128
- partner: int32 [32], replicated, may hold values from 0 to 31, as said below
- pair_weight: float32 [32], P(('fsdp', 'dp')), may hold values from 0.25 to 27
- norm_gain: float32 [3584], replicated, may hold values from 0.5 to 1.5
- qkv_weight: bfloat16 [3584, 4608], P('fsdp'), may hold values from -0.09375 to 0.09375
- qkv_bias: float32 [4608], replicated, may hold values from -40 to 40
- out_weight: bfloat16 [3584, 3584], P(None, 'fsdp'), may hold values from -0.09375 to 0.09375
- final_gain: float32 [3584], replicated, may hold values from 0.5 to 1.5
- value_head: float32 [3584], replicated, may hold values from -0.09375 to 0.09375
Outputs:
- hidden: bfloat16 [32, 128, 3584], P(('fsdp', 'dp'))
- margins: float32 [32], P(('fsdp', 'dp'))
- loss: float32 [], replicated
Inputs may be any that keep to these rules, and one draw needn't show every extreme that they name: partner[partner[i]] = i and partner[i] != i.
All inputs are finite; a program needn't handle non-finite values.
Results may differ from a plain program's by a relative error of at most 0.013.
The roundings to bfloat16 on the way count: a program that leaves them out, or rounds other values in their place, can miss the bound.
Values may be sent and summed in bfloat16 or wider, within the bound.
A program may use at most 128 MiB of HBM per device.

v0:
```python
import functools

import jax
import jax.numpy as jnp
import numpy as np
from jax import lax
from jax.experimental import pallas as pl
from jax.experimental.pallas import tpu as pltpu
from jax.sharding import PartitionSpec as P

QUERY_HEADS = 28
KEY_VALUE_HEADS = 4
HEAD_SIZE = 128
QUERY_FEATURES = 3584
KEY_FEATURES = 512


def rms_scale(value_rows, gain):
    return (
        value_rows
        * lax.rsqrt(jnp.mean(value_rows * value_rows, axis=-1, keepdims=True) + 1e-06)
        * gain
    )


def apply_rotary(heads, length_rows):
    half = HEAD_SIZE // 2
    positions = jnp.arange(length_rows, dtype=jnp.float32)
    freqs = jnp.exp(
        -(2.0 * jnp.arange(half, dtype=jnp.float32) / HEAD_SIZE) * jnp.log(jnp.float32(1000000.0))
    )
    angles = positions[:, None] * freqs[None, :]
    cosine = jnp.cos(angles)
    sine = jnp.sin(angles)
    first = heads[..., :half]
    second = heads[..., half:]
    return jnp.concatenate(
        [first * cosine - second * sine, second * cosine + first * sine], axis=-1
    )


def attend(query_key_value, group_lengths, query_heads, key_value_heads):
    seq_count, length_rows, _ = query_key_value.shape
    query_width = query_heads * HEAD_SIZE
    key_width = key_value_heads * HEAD_SIZE
    query_rows = (
        query_key_value[..., :query_width]
        .reshape(seq_count, length_rows, query_heads, HEAD_SIZE)
        .transpose(0, 2, 1, 3)
    )
    key_rows = (
        query_key_value[..., query_width : query_width + key_width]
        .reshape(seq_count, length_rows, key_value_heads, HEAD_SIZE)
        .transpose(0, 2, 1, 3)
    )
    value_rows = (
        query_key_value[..., query_width + key_width :]
        .reshape(seq_count, length_rows, key_value_heads, HEAD_SIZE)
        .transpose(0, 2, 1, 3)
        .astype(jnp.bfloat16)
    )
    query_rows = (
        apply_rotary(query_rows, length_rows)
        .astype(jnp.bfloat16)
        .reshape(seq_count, key_value_heads, query_heads // key_value_heads, length_rows, HEAD_SIZE)
    )
    key_rows = apply_rotary(key_rows, length_rows).astype(jnp.bfloat16)
    scores = jnp.einsum(
        "bgqtd,bgsd->bgqts", query_rows, key_rows, preferred_element_type=jnp.float32
    ) / jnp.sqrt(jnp.float32(HEAD_SIZE))
    places = jnp.arange(length_rows, dtype=jnp.int32)
    causal = places[None, :] <= places[:, None]
    usable = places[None, :] < group_lengths[:, None]
    allowed = causal[None, :, :] & usable[:, None, :]
    scores = jnp.where(allowed[:, None, None, :, :], scores, jnp.float32(-1e30))
    highest = jnp.max(scores, axis=-1, keepdims=True)
    expd = jnp.exp(scores - highest)
    probs = (expd / jnp.sum(expd, axis=-1, keepdims=True)).astype(jnp.bfloat16)
    mixed = jnp.einsum("bgqts,bgsd->bgqtd", probs, value_rows, preferred_element_type=jnp.float32)
    mixed = mixed.reshape(seq_count, query_heads, length_rows, HEAD_SIZE).transpose(0, 2, 1, 3)
    return mixed.reshape(seq_count * length_rows, query_width).astype(jnp.bfloat16)


UP, DOWN, ACROSS = 0, 1, 2


def rotary_tables(length_rows):
    half = HEAD_SIZE // 2
    freqs = 1000000.0 ** (-2.0 * np.arange(half) / HEAD_SIZE)
    angles = np.arange(length_rows)[:, None] * freqs[None, :]
    cosine, sine = np.cos(angles), np.sin(angles)
    return (
        np.concatenate([cosine, cosine], axis=1).astype(np.float32),
        np.concatenate([-sine, sine], axis=1).astype(np.float32),
    )


def layer_kernel(
    shards,
    groups,
    tokens,
    qkv_weight,
    out_weight,
    length,
    pair_weight,
    partner,
    norm_gain_flat,
    final_gain_flat,
    value_head_flat,
    qkv_bias_flat,
    cosine,
    sine,
    hidden,
    margin_out,
    loss_out,
    qkv_full,
    out_full,
    tok_all,
    len_tile,
    len_all,
    normed,
    qkv_rows,
    attn,
    own,
    part_out,
    part_in,
    score_tile,
    score_all,
    partner_rows,
    norm_gain,
    final_gain,
    value_head,
    qkv_bias,
    local_sem,
    recv_sem,
    send_sem,
    tok_send,
    tok_recv,
    len_send,
    len_recv,
    part_send,
    part_recv,
    score_send,
    score_recv,
):
    line = shards // 2
    f = lax.axis_index("fsdp")
    g = lax.axis_index("dp")
    z = f // 2
    y = f % 2
    even = z % 2 == 0
    seq_rows = tokens.shape[0]
    depth = qkv_weight.shape[0]
    width = tok_all.shape[2]
    query_cols = QUERY_FEATURES // groups
    key_cols = KEY_FEATURES // groups
    heads = query_cols // HEAD_SIZE
    half_depth = depth // 2
    half_out = out_weight.shape[0] // 2
    has_up = z < line - 1
    has_down = z > 0

    def slot(m, c, s):
        if m == 0:
            return qkv_full.at[pl.ds(pl.multiple_of(s * depth + c * half_depth, 32), half_depth)]
        return out_full.at[s, pl.ds(c * half_out, half_out)]

    locals_ = [[[], []], [[], []]]
    count = 0
    for c in range(2):
        rows = pl.ds(c * half_depth, half_depth)
        there = slot(0, c, f)
        for start, size, to in (
            (g * query_cols, query_cols, 0),
            (QUERY_FEATURES + g * key_cols, key_cols, query_cols),
            (QUERY_FEATURES + KEY_FEATURES + g * key_cols, key_cols, query_cols + key_cols),
        ):
            locals_[0][c].append(
                pltpu.make_async_copy(
                    qkv_weight.at[rows, pl.ds(pl.multiple_of(start, 128), size)],
                    there.at[:, pl.ds(to, size)],
                    local_sem.at[count],
                )
            )
            count += 1
    for c in range(2):
        locals_[1][c].append(
            pltpu.make_async_copy(
                out_weight.at[
                    pl.ds(c * half_out, half_out),
                    pl.ds(pl.multiple_of(g * query_cols, 128), query_cols),
                ],
                slot(1, c, f),
                local_sem.at[count],
            )
        )
        count += 1
    tok_local = pltpu.make_async_copy(tokens, tok_all.at[g], local_sem.at[count])
    len_tile[...] = jnp.full(len_tile.shape, length[0], jnp.int32)
    len_all[g] = len_tile[...]
    for m in range(2):
        for c in range(2):
            for copy in locals_[m][c]:
                copy.start()
    tok_local.start()
    vectors = [
        pltpu.make_async_copy(flat, row.at[0], local_sem.at[count + 1 + i])
        for i, (flat, row) in enumerate(
            (
                (norm_gain_flat, norm_gain),
                (final_gain_flat, final_gain),
                (value_head_flat, value_head),
                (qkv_bias_flat, qkv_bias),
            )
        )
    ]
    for copy in vectors:
        copy.start()

    barrier = pltpu.get_barrier_semaphore()
    across = 2 * z + 1 - y
    everyone = shards * groups
    me = f * groups + g

    @pl.loop(1, everyone)
    def _(i):
        other = lax.rem(me + i, everyone)
        pl.semaphore_signal(
            barrier, inc=1, device_id={"fsdp": other // groups, "dp": lax.rem(other, groups)}
        )

    peers = [lax.rem(g + i, groups) for i in range(1, groups)]
    pl.semaphore_wait(barrier, everyone - 1)

    started = []

    def send(cond, way, m, c, s):
        target = (f + 2, f - 2, across)[way]
        copy = pltpu.make_async_remote_copy(
            src_ref=slot(m, c, s),
            dst_ref=slot(m, c, s),
            send_sem=send_sem.at[way, m, c, s],
            recv_sem=recv_sem.at[m, c, s],
            device_id={"fsdp": target},
        )
        started.append((cond, copy))
        if cond is None:
            copy.start()
        else:
            pl.when(cond)(copy.start)

    def arrived(m, c, s):
        pltpu.make_async_copy(slot(m, c, s), slot(m, c, s), recv_sem.at[m, c, s]).wait()

    def own_line(m, c):
        send(has_up, UP, m, c, f)
        send(has_down, DOWN, m, c, f)

    def line_step(m, k):
        for c in range(2):
            below = z - k
            above = z + k
            s_below = 2 * jnp.maximum(below, 0) + y
            s_above = 2 * jnp.minimum(above, line - 1) + y

            @pl.when(below >= 0)
            def _():
                arrived(m, c, s_below)

            send((below >= 0) & has_up, UP, m, c, s_below)
            if k > 1 or c == 0:
                send(below >= 0, ACROSS, m, c, s_below)
            else:
                send((below >= 0) & even, ACROSS, m, c, s_below)

            @pl.when(above < line)
            def _():
                arrived(m, c, s_above)

            send((above < line) & has_down, DOWN, m, c, s_above)
            if k > 1 or c == 0:
                send(above < line, ACROSS, m, c, s_above)
            else:
                send((above < line) & jnp.logical_not(even), ACROSS, m, c, s_above)

    def half_step(m):
        arrived(m, 1, across)
        send(even, UP, m, 1, across)
        send(jnp.logical_not(even), DOWN, m, 1, across)

    for c in range(2):
        for copy in locals_[0][c]:
            copy.wait()
        own_line(0, c)
        send(None, ACROSS, 0, c, f)
    small = []
    for peer in peers:
        for source, dest, ss, rs in (
            (tokens, tok_all, tok_send, tok_recv),
            (len_tile, len_all, len_send, len_recv),
        ):
            copy = pltpu.make_async_remote_copy(
                src_ref=source,
                dst_ref=dest.at[g],
                send_sem=ss.at[peer],
                recv_sem=rs.at[g],
                device_id={"dp": peer},
            )
            copy.start()
            small.append(copy)

    line_step(0, 1)
    for k in range(2, line - 1):
        line_step(0, k)
    half_step(0)
    for c in range(2):
        for copy in locals_[1][c]:
            copy.wait()
        own_line(1, c)

    tok_local.wait()
    for copy in vectors:
        copy.wait()
    for peer in peers:
        pltpu.make_async_copy(tok_all.at[peer], tok_all.at[peer], tok_recv.at[peer]).wait()
        pltpu.make_async_copy(len_all.at[peer], len_all.at[peer], len_recv.at[peer]).wait()

    norm_rows = 16
    for j in range(groups):

        @pl.loop(0, seq_rows // norm_rows)
        def _(i):
            at = pl.multiple_of(i * norm_rows, norm_rows)
            rows = tok_all[j, pl.ds(at, norm_rows), :].astype(jnp.float32)
            scale = lax.rsqrt(jnp.mean(rows * rows, axis=-1, keepdims=True) + 1e-06)
            normed[pl.ds(pl.multiple_of(j * seq_rows + at, norm_rows), norm_rows), :] = (
                rows * scale * norm_gain[...]
            ).astype(jnp.bfloat16)

    line_step(0, line - 1)
    for c in range(2):
        send(None, ACROSS, 1, c, f)

    def across_wait(m, k):
        for c in range(2):
            if k == 0:
                if c == 0:
                    arrived(m, c, across)
                continue
            for there, ok in ((z - k, z - k >= 0), (z + k, z + k < line)):
                s = 2 * jnp.clip(there, 0, line - 1) + 1 - y

                @pl.when(ok)
                def _():
                    arrived(m, c, s)

    for k in range(line):
        across_wait(0, k)

    tile = 3 * HEAD_SIZE

    @pl.loop(0, (query_cols + 2 * key_cols) // tile)
    def _(t):
        cols = pl.ds(pl.multiple_of(t * tile, tile), tile)
        qkv_rows[:, cols] = jnp.dot(
            normed[...], qkv_full[:, cols], preferred_element_type=jnp.float32
        )

    def head_rows(j, column, bias_at):
        rows = qkv_rows[pl.ds(pl.multiple_of(j * seq_rows, seq_rows), seq_rows), pl.ds(column, HEAD_SIZE)]
        return rows + qkv_bias[:, pl.ds(pl.multiple_of(bias_at, HEAD_SIZE), HEAD_SIZE)]

    def rotate(rows):
        return (
            rows * cosine[...] + pltpu.roll(rows, HEAD_SIZE // 2, 1) * sine[...]
        ).astype(jnp.bfloat16)

    key_heads = key_cols // HEAD_SIZE
    share = heads // key_heads

    def attend_sequence(j):
        query_place = lax.broadcasted_iota(jnp.int32, (seq_rows, seq_rows), 0)
        key_place = lax.broadcasted_iota(jnp.int32, (seq_rows, seq_rows), 1)
        allowed = (key_place <= query_place) & (key_place < len_all[j, 0:1, :])
        at = pl.ds(pl.multiple_of(j * seq_rows, seq_rows), seq_rows)
        for kh in range(key_heads):
            offset = kh * HEAD_SIZE
            key = rotate(
                head_rows(j, query_cols + offset, QUERY_FEATURES + g * key_cols + offset)
            )
            value = head_rows(
                j,
                query_cols + key_cols + offset,
                QUERY_FEATURES + KEY_FEATURES + g * key_cols + offset,
            ).astype(jnp.bfloat16)
            for h in range(kh * share, (kh + 1) * share):
                query = rotate(head_rows(j, h * HEAD_SIZE, g * query_cols + h * HEAD_SIZE))
                scores = lax.dot_general(
                    query, key, (((1,), (1,)), ((), ())), preferred_element_type=jnp.float32
                ) / np.float32(np.sqrt(HEAD_SIZE))
                scores = jnp.where(allowed, scores, jnp.float32(-1e30))
                expd = jnp.exp(scores - jnp.max(scores, axis=-1, keepdims=True))
                probs = (expd / jnp.sum(expd, axis=-1, keepdims=True)).astype(jnp.bfloat16)
                attn[at, h * HEAD_SIZE : (h + 1) * HEAD_SIZE] = jnp.dot(
                    probs, value, preferred_element_type=jnp.float32
                ).astype(jnp.bfloat16)

    pl.loop(0, groups // 2)(attend_sequence)
    line_step(1, 1)
    pl.loop(groups // 2, groups)(attend_sequence)

    def part_copy(peer, s):
        return pltpu.make_async_remote_copy(
            src_ref=part_out.at[s, pl.ds(pl.multiple_of(peer * seq_rows, seq_rows), seq_rows)],
            dst_ref=part_in.at[g, s],
            send_sem=part_send.at[peer, s],
            recv_sem=part_recv.at[g, s],
            device_id={"dp": peer},
        )

    def project(s):
        result = lax.dot_general(
            attn[...],
            out_full[s],
            (((1,), (1,)), ((), ())),
            preferred_element_type=jnp.float32,
        )
        part_out[s] = result.astype(jnp.bfloat16)
        for j in range(groups):

            @pl.when(g == j)
            def _():
                own[s] = result[j * seq_rows : (j + 1) * seq_rows]

        for peer in peers:
            part_copy(peer, s).start()

    def project_places(k, side):
        @pl.loop(0, 1 if k == 0 else 2)
        def _(i):
            there = z + (2 * i - 1) * k

            @pl.when((there >= 0) & (there < line))
            def _():
                project(2 * there + side)

    for k in range(2, line - 1):
        line_step(1, k)
    half_step(1)
    across_wait(1, 0)

    @pl.loop(0, 2)
    def _(side):
        project(2 * z + side)

    project_places(1, y)
    line_step(1, line - 1)
    for k in range(2, line):
        project_places(k, y)
    for k in range(1, line):
        across_wait(1, k)
        project_places(k, 1 - y)

    @pl.loop(0, shards)
    def _(s):
        for peer in peers:
            pltpu.make_async_copy(
                part_in.at[peer, s], part_in.at[peer, s], part_recv.at[peer, s]
            ).wait()

    block = 32
    out_cols = own.shape[2]

    @pl.loop(0, seq_rows // block)
    def _(i):
        at = pl.ds(pl.multiple_of(i * block, block), block)
        for p in range(shards // 2):
            sums = []
            for s in (2 * p, 2 * p + 1):
                total = own[s, at]
                for peer in peers:
                    total += part_in[peer, s, at].astype(jnp.float32)
                sums.append(total)
            cols = slice(2 * p * out_cols, 2 * (p + 1) * out_cols)
            hidden[at, cols] = (
                tok_all[g, at, cols].astype(jnp.float32) + jnp.concatenate(sums, axis=1)
            ).astype(jnp.bfloat16)

    place = lax.broadcasted_iota(jnp.int32, len_tile.shape, 1)
    pick = (place == len_tile[...] - 1).astype(jnp.bfloat16)
    last = jnp.dot(pick, hidden[...], preferred_element_type=jnp.float32)
    scale = lax.rsqrt(jnp.mean(last * last, axis=-1, keepdims=True) + 1e-06)
    score = jnp.sum(last * scale * final_gain[...] * value_head[...], axis=-1, keepdims=True)
    first_row = lax.broadcasted_iota(jnp.int32, score_tile.shape, 0) == 0
    score_tile[...] = jnp.where(first_row, score, jnp.full(score_tile.shape, pair_weight[0]))
    score_all[me] = score_tile[...]

    def score_copy(i):
        other = lax.rem(me + i, everyone)
        return pltpu.make_async_remote_copy(
            src_ref=score_tile,
            dst_ref=score_all.at[me],
            send_sem=score_send.at[other],
            recv_sem=score_recv.at[me],
            device_id={"fsdp": other // groups, "dp": lax.rem(other, groups)},
        )

    @pl.loop(1, everyone)
    def _(i):
        score_copy(i).start()

    @pl.loop(0, everyone)
    def _(i):
        partner_rows[pl.ds(i, 1), :] = jnp.full((1, HEAD_SIZE), partner[i], jnp.int32)

    @pl.loop(1, everyone)
    def _(i):
        other = lax.rem(me + i, everyone)
        pltpu.make_async_copy(
            score_all.at[other], score_all.at[other], score_recv.at[other]
        ).wait()

    scores = score_all[:, 0, :]
    weights = score_all[:, 1, :]
    row = lax.broadcasted_iota(jnp.int32, scores.shape, 0)
    lane = lax.broadcasted_iota(jnp.int32, scores.shape, 1)
    partners = partner_rows[...]
    score_row = jnp.sum(jnp.where(row == lane, scores, 0.0), axis=0, keepdims=True)
    others = jnp.sum(jnp.where(partners == lane, score_row, 0.0), axis=1, keepdims=True)
    margins = jnp.where(row < partners, scores - others, others - scores)
    softplus = jnp.maximum(-margins, 0.0) + jnp.log1p(jnp.exp(-jnp.abs(margins)))
    first_lane = lane == 0
    margin_out[0] = jnp.sum(jnp.where(first_lane & (row == me), margins, 0.0))
    loss_out[0] = jnp.sum(jnp.where(first_lane, weights * softplus, 0.0)) / everyone

    for cond, copy in started:
        if cond is None:
            copy.wait_send()
        else:
            pl.when(cond)(copy.wait_send)
    for copy in small:
        copy.wait_send()

    @pl.loop(0, shards)
    def _(s):
        for peer in peers:
            part_copy(peer, s).wait_send()

    @pl.loop(1, everyone)
    def _(i):
        score_copy(i).wait_send()


def layer_fits(shards, groups, tokens, qkv_weight, out_weight):
    return (
        shards % 4 == 0
        and shards >= 8
        and qkv_weight.shape[0] % 32 == 0
        and KEY_VALUE_HEADS % groups == 0
        and tokens.shape[1] == HEAD_SIZE
        and groups % 2 == 0
        and shards * groups <= HEAD_SIZE
        and out_weight.shape[1] % 64 == 0
    )


def layer(
    tokens,
    lengths,
    partner,
    pair_weight,
    norm_gain,
    qkv_weight,
    qkv_bias,
    out_weight,
    final_gain,
    value_head,
):
    shards, groups = lax.axis_size("fsdp"), lax.axis_size("dp")
    _, seq_rows, width = tokens.shape
    depth = qkv_weight.shape[0]
    out_cols = out_weight.shape[1]
    query_cols = QUERY_FEATURES // groups
    key_cols = KEY_FEATURES // groups
    all_cols = query_cols + 2 * key_cols
    rows = groups * seq_rows
    cosine, sine = rotary_tables(seq_rows)
    everyone = shards * groups
    dma = pltpu.SemaphoreType.DMA
    vmem = pl.BlockSpec(memory_space=pltpu.VMEM)
    anywhere = pl.BlockSpec(memory_space=pl.ANY)
    bf16, f32 = jnp.bfloat16, jnp.float32
    scalar = pl.BlockSpec(memory_space=pltpu.SMEM)
    hidden, margin, loss = pl.pallas_call(
        functools.partial(layer_kernel, shards, groups),
        out_shape=(
            jax.ShapeDtypeStruct((seq_rows, width), bf16),
            jax.ShapeDtypeStruct((1,), f32),
            jax.ShapeDtypeStruct((1,), f32),
        ),
        in_specs=[anywhere] * 3 + [scalar] * 3 + [anywhere] * 4 + [vmem] * 2,
        out_specs=(vmem, scalar, scalar),
        scratch_shapes=[
            pltpu.VMEM((shards * depth, all_cols), bf16),
            pltpu.VMEM((shards, out_cols, query_cols), bf16),
            pltpu.VMEM((groups, seq_rows, width), bf16),
            pltpu.VMEM((8, seq_rows), jnp.int32),
            pltpu.VMEM((groups, 8, seq_rows), jnp.int32),
            pltpu.VMEM((rows, width), bf16),
            pltpu.VMEM((rows, all_cols), f32),
            pltpu.VMEM((rows, query_cols), bf16),
            pltpu.VMEM((shards, seq_rows, out_cols), f32),
            pltpu.VMEM((shards, rows, out_cols), bf16),
            pltpu.VMEM((groups, shards, seq_rows, out_cols), bf16),
            pltpu.VMEM((8, HEAD_SIZE), f32),
            pltpu.VMEM((everyone, 8, HEAD_SIZE), f32),
            pltpu.VMEM((everyone, HEAD_SIZE), jnp.int32),
            pltpu.VMEM((1, width), f32),
            pltpu.VMEM((1, width), f32),
            pltpu.VMEM((1, width), f32),
            pltpu.VMEM((1, qkv_bias.shape[0]), f32),
            dma((13,)),
            dma((2, 2, shards)),
            dma((3, 2, 2, shards)),
            dma((groups,)),
            dma((groups,)),
            dma((groups,)),
            dma((groups,)),
            dma((groups, shards)),
            dma((groups, shards)),
            dma((everyone,)),
            dma((everyone,)),
        ],
        compiler_params=pltpu.CompilerParams(
            collective_id=0, has_side_effects=True, vmem_limit_bytes=60 * 1024 * 1024
        ),
    )(
        tokens[0],
        qkv_weight,
        out_weight.T,
        lengths,
        pair_weight,
        partner,
        norm_gain,
        final_gain,
        value_head,
        qkv_bias,
        jnp.asarray(cosine),
        jnp.asarray(sine),
    )
    return hidden[None], margin, loss.reshape(())


def projected_by_gathers(
    tokens,
    lengths,
    norm_gain,
    qkv_weight,
    qkv_bias,
    out_weight,
):
    sequence = tokens[0]
    length_rows = sequence.shape[0]
    width = sequence.shape[1]
    normed = rms_scale(sequence.astype(jnp.float32), norm_gain).astype(jnp.bfloat16)
    query_group_count = lax.axis_size("dp")
    group_index = lax.axis_index("dp")
    query_heads = QUERY_HEADS // query_group_count
    key_value_heads = KEY_VALUE_HEADS // query_group_count
    query_cols = query_heads * HEAD_SIZE
    key_cols = key_value_heads * HEAD_SIZE
    group_normed, group_lengths = (
        lax.all_gather(normed[None], "dp", axis=0, tiled=True),
        lax.all_gather(lengths, "dp", axis=0, tiled=True),
    )
    seq_count = group_normed.shape[0]
    flat = group_normed.reshape(seq_count * length_rows, width)
    qkv_cols = jnp.concatenate(
        [
            lax.dynamic_slice_in_dim(qkv_weight, group_index * query_cols, query_cols, 1),
            lax.dynamic_slice_in_dim(
                qkv_weight, QUERY_FEATURES + group_index * key_cols, key_cols, 1
            ),
            lax.dynamic_slice_in_dim(
                qkv_weight, QUERY_FEATURES + KEY_FEATURES + group_index * key_cols, key_cols, 1
            ),
        ],
        axis=1,
    )
    bias_cols = jnp.concatenate(
        [
            lax.dynamic_slice_in_dim(qkv_bias, group_index * query_cols, query_cols, 0),
            lax.dynamic_slice_in_dim(
                qkv_bias, QUERY_FEATURES + group_index * key_cols, key_cols, 0
            ),
            lax.dynamic_slice_in_dim(
                qkv_bias, QUERY_FEATURES + KEY_FEATURES + group_index * key_cols, key_cols, 0
            ),
        ],
        axis=0,
    )
    out_rows = lax.dynamic_slice_in_dim(out_weight, group_index * query_cols, query_cols, 0)
    qkv_full, out_full = (
        lax.all_gather(qkv_cols, "fsdp", axis=0, tiled=True),
        lax.all_gather(out_rows, "fsdp", axis=1, tiled=True),
    )
    query_key_value = jnp.dot(flat, qkv_full, preferred_element_type=jnp.float32) + bias_cols
    attn = attend(
        query_key_value.reshape(seq_count, length_rows, -1),
        group_lengths,
        query_heads,
        key_value_heads,
    )
    return lax.psum_scatter(
        jnp.dot(attn, out_full, preferred_element_type=jnp.float32),
        "dp",
        scatter_dimension=0,
        tiled=True,
    )


def per_device(
    tokens,
    lengths,
    partner,
    pair_weight,
    norm_gain,
    qkv_weight,
    qkv_bias,
    out_weight,
    final_gain,
    value_head,
):
    if layer_fits(lax.axis_size("fsdp"), lax.axis_size("dp"), tokens, qkv_weight, out_weight):
        return layer(
            tokens,
            lengths,
            partner,
            pair_weight,
            norm_gain,
            qkv_weight,
            qkv_bias,
            out_weight,
            final_gain,
            value_head,
        )
    sequence = tokens[0]
    length = lengths[0]
    projected = projected_by_gathers(tokens, lengths, norm_gain, qkv_weight, qkv_bias, out_weight)
    hidden = (sequence.astype(jnp.float32) + projected).astype(jnp.bfloat16)
    last = lax.dynamic_slice_in_dim(hidden, length - 1, 1, 0)[0].astype(jnp.float32)
    score = jnp.sum(rms_scale(last, final_gain) * value_head)
    everyone, weights_all = (
        lax.all_gather(score.reshape(1), ("fsdp", "dp"), axis=0, tiled=True),
        lax.all_gather(pair_weight, ("fsdp", "dp"), axis=0, tiled=True),
    )
    total_seqs = everyone.shape[0]
    mine = lax.axis_index(("fsdp", "dp"))
    index_all = jnp.arange(total_seqs, dtype=jnp.int32)
    my_partner = jnp.sum(jnp.where(index_all == mine, partner, 0))
    other = jnp.sum(jnp.where(index_all == my_partner, everyone, jnp.float32(0.0)))
    margin = jnp.where(mine < my_partner, score - other, other - score)
    matches = partner[:, None] == index_all[None, :]
    others_all = jnp.sum(jnp.where(matches, everyone[None, :], jnp.float32(0.0)), axis=1)
    margins_all = jnp.where(index_all < partner, everyone - others_all, others_all - everyone)
    loss = jnp.sum(weights_all * jax.nn.softplus(-margins_all)) / total_seqs
    return (hidden[None], margin.reshape(1), loss)


def solution(mesh):
    return jax.shard_map(
        per_device,
        mesh=mesh,
        in_specs=(
            P(("fsdp", "dp"), None, None),
            P(("fsdp", "dp")),
            P(),
            P(("fsdp", "dp")),
            P(),
            P("fsdp", None),
            P(),
            P(None, "fsdp"),
            P(),
            P(),
        ),
        out_specs=(P(("fsdp", "dp"), None, None), P(("fsdp", "dp")), P()),
        check_vma=False,
    )
```

profile of v0, /device:TPU:0, one launch (start us, length us, event | category | flops | bytes accessed | tf_op | source)
XLA Modules:
  0.0 185.7 jit_solution(12749694540796976451)
XLA Ops:
  1.9 178.1 %shard_map.139 = (bf16[128,3584]{1,0:T(8,128)(2,1)}, f32[1]{0:T(128)}, f32[1]{0:T(128)}) custom-call(bf16[128,3584]{1,0:T(8,128)(2,1)} %bitcast.5, bf16[448,4608]{1,0:T(8,128)(2,1)} %qkv_weight.1, bf16[448,3584]{1,0:T(8,128)(2,1)} %bitcast.4, s32[1]{0:T(128)S(6)} %copy.18.length, f32[1]{0:T(128)S(6)} %copy.19.pair_weight, s32[32]{0:T(128)} %partner.1, ...), custom_call_target="tpu_custom_call" | custom-call | tf_op jit(solution)/shard_map/pallas_call | solution.py:594
  180.0 2.2 %copy.20 = bf16[1,128,3584]{2,1,0:T(8,128)(2,1)} copy(bf16[1,128,3584]{2,1,0:T(8,128)(2,1)} %bitcast.6) | data formatting | bytes 1835008
where the time goes:
time: 186 us
  Pallas kernels  178 us (96%)
  between operations  5.48 us (3%)
  local copies, waits for them, and re-layouts  2.16 us (1%)
    pallas_call x1, Pallas kernels, layer(): pl.pallas_call(functools.partial(layer_kernel, shards, groups), out_shape...  178 us

commit v1 on v0

--- a/solution.py
+++ b/solution.py
@@ -81,7 +81,7 @@
     return mixed.reshape(seq_count * length_rows, query_width).astype(jnp.bfloat16)
 
 
-UP, DOWN, ACROSS = 0, 1, 2
+UP, DOWN, PARTNER = 0, 1, 2
 
 
 def rotary_tables(length_rows):
@@ -110,12 +110,14 @@
     qkv_bias_flat,
     cosine,
     sine,
-    hidden,
+    hidden_out,
     margin_out,
     loss_out,
     qkv_full,
     out_full,
-    tok_all,
+    cross_qkv,
+    cross_out,
+    tok_own,
     len_tile,
     len_all,
     normed,
@@ -124,6 +126,8 @@
     own,
     part_out,
     part_in,
+    hidden,
+    stats,
     score_tile,
     score_all,
     partner_rows,
@@ -134,6 +138,7 @@
     local_sem,
     recv_sem,
     send_sem,
+    cross_send,
     tok_send,
     tok_recv,
     len_send,
@@ -142,83 +147,97 @@
     part_recv,
     score_send,
     score_recv,
+    hidden_sem,
 ):
     line = shards // 2
     f = lax.axis_index("fsdp")
     g = lax.axis_index("dp")
     z = f // 2
     y = f % 2
-    even = z % 2 == 0
+    x = g // 2
+    core = g % 2
     seq_rows = tokens.shape[0]
+    width = tokens.shape[1]
     depth = qkv_weight.shape[0]
-    width = tok_all.shape[2]
+    out_cols = out_weight.shape[0]
     query_cols = QUERY_FEATURES // groups
     key_cols = KEY_FEATURES // groups
     heads = query_cols // HEAD_SIZE
-    half_depth = depth // 2
-    half_out = out_weight.shape[0] // 2
+    quarter = depth // 4
+    out_quarter = out_cols // 4
     has_up = z < line - 1
     has_down = z > 0
-
-    def slot(m, c, s):
+    team = 2 * x + y
+    across_team = 2 * x + 1 - y
+    across = 2 * z + 1 - y
+    x_peer = 2 * (1 - x) + core
+    team_ids = ({"dp": x_peer}, {"fsdp": across}, {"fsdp": across, "dp": x_peer})
+    way_ids = ({"fsdp": f + 2}, {"fsdp": f - 2}, {"dp": 2 * x + 1 - core})
+
+    def slot(m, s, k):
         if m == 0:
-            return qkv_full.at[pl.ds(pl.multiple_of(s * depth + c * half_depth, 32), half_depth)]
-        return out_full.at[s, pl.ds(c * half_out, half_out)]
-
-    locals_ = [[[], []], [[], []]]
+            return qkv_full.at[pl.ds(pl.multiple_of(s * depth + k * quarter, 16), quarter)]
+        return out_full.at[s, pl.ds(pl.multiple_of(k * out_quarter, 16), out_quarter)]
+
     count = 0
-    for c in range(2):
-        rows = pl.ds(c * half_depth, half_depth)
-        there = slot(0, c, f)
-        for start, size, to in (
-            (g * query_cols, query_cols, 0),
-            (QUERY_FEATURES + g * key_cols, key_cols, query_cols),
-            (QUERY_FEATURES + KEY_FEATURES + g * key_cols, key_cols, query_cols + key_cols),
-        ):
-            locals_[0][c].append(
-                pltpu.make_async_copy(
-                    qkv_weight.at[rows, pl.ds(pl.multiple_of(start, 128), size)],
-                    there.at[:, pl.ds(to, size)],
-                    local_sem.at[count],
-                )
+
+    def local(source, dest):
+        nonlocal count
+        copy = pltpu.make_async_copy(source, dest, local_sem.at[count])
+        count += 1
+        copy.start()
+        return copy
+
+    def qkv_parts(k, owner, dest):
+        rows = pl.ds(pl.multiple_of(k * quarter, 16), quarter)
+        return [
+            local(
+                qkv_weight.at[rows, pl.ds(pl.multiple_of(start, 128), size)],
+                dest.at[:, pl.ds(to, size)],
             )
-            count += 1
-    for c in range(2):
-        locals_[1][c].append(
-            pltpu.make_async_copy(
-                out_weight.at[
-                    pl.ds(c * half_out, half_out),
-                    pl.ds(pl.multiple_of(g * query_cols, 128), query_cols),
-                ],
-                slot(1, c, f),
-                local_sem.at[count],
+            for start, size, to in (
+                (owner * query_cols, query_cols, 0),
+                (QUERY_FEATURES + owner * key_cols, key_cols, query_cols),
+                (QUERY_FEATURES + KEY_FEATURES + owner * key_cols, key_cols, query_cols + key_cols),
             )
-        )
-        count += 1
-    tok_local = pltpu.make_async_copy(tokens, tok_all.at[g], local_sem.at[count])
+        ]
+
+    own_loads, cross_loads = [], []
+    for j in range(2):
+        k = 2 * j + core
+        own_loads.append(qkv_parts(k, team, slot(0, f, k)))
+        cross_loads.append(qkv_parts(k, across_team, cross_qkv.at[j]))
+    tok_local = local(tokens, tok_own)
+    vectors = [
+        local(flat, row.at[0, pl.ds(0, flat.shape[0])])
+        for flat, row in (
+            (norm_gain_flat, norm_gain),
+            (final_gain_flat, final_gain),
+            (value_head_flat, value_head),
+            (qkv_bias_flat, qkv_bias),
+        )
+    ]
+    late_loads = []
+    for j in range(2):
+        k = 2 * j + 1 - core
+        late_loads.extend(qkv_parts(k, team, slot(0, f, k)))
+    out_own = local(
+        out_weight.at[:, pl.ds(pl.multiple_of(team * query_cols, 128), query_cols)], out_full.at[f]
+    )
+    out_cross = [
+        local(
+            out_weight.at[
+                pl.ds(pl.multiple_of((2 * j + core) * out_quarter, 16), out_quarter),
+                pl.ds(pl.multiple_of(across_team * query_cols, 128), query_cols),
+            ],
+            cross_out.at[j],
+        )
+        for j in range(2)
+    ]
     len_tile[...] = jnp.full(len_tile.shape, length[0], jnp.int32)
-    len_all[g] = len_tile[...]
-    for m in range(2):
-        for c in range(2):
-            for copy in locals_[m][c]:
-                copy.start()
-    tok_local.start()
-    vectors = [
-        pltpu.make_async_copy(flat, row.at[0], local_sem.at[count + 1 + i])
-        for i, (flat, row) in enumerate(
-            (
-                (norm_gain_flat, norm_gain),
-                (final_gain_flat, final_gain),
-                (value_head_flat, value_head),
-                (qkv_bias_flat, qkv_bias),
-            )
-        )
-    ]
-    for copy in vectors:
-        copy.start()
+    len_all[0] = len_tile[...]
 
     barrier = pltpu.get_barrier_semaphore()
-    across = 2 * z + 1 - y
     everyone = shards * groups
     me = f * groups + g
 
@@ -229,146 +248,190 @@
             barrier, inc=1, device_id={"fsdp": other // groups, "dp": lax.rem(other, groups)}
         )
 
-    peers = [lax.rem(g + i, groups) for i in range(1, groups)]
     pl.semaphore_wait(barrier, everyone - 1)
 
-    started = []
-
-    def send(cond, way, m, c, s):
-        target = (f + 2, f - 2, across)[way]
-        copy = pltpu.make_async_remote_copy(
-            src_ref=slot(m, c, s),
-            dst_ref=slot(m, c, s),
-            send_sem=send_sem.at[way, m, c, s],
-            recv_sem=recv_sem.at[m, c, s],
-            device_id={"fsdp": target},
-        )
-        started.append((cond, copy))
-        if cond is None:
-            copy.start()
-        else:
-            pl.when(cond)(copy.start)
-
-    def arrived(m, c, s):
-        pltpu.make_async_copy(slot(m, c, s), slot(m, c, s), recv_sem.at[m, c, s]).wait()
-
-    def own_line(m, c):
-        send(has_up, UP, m, c, f)
-        send(has_down, DOWN, m, c, f)
-
-    def line_step(m, k):
-        for c in range(2):
-            below = z - k
-            above = z + k
-            s_below = 2 * jnp.maximum(below, 0) + y
-            s_above = 2 * jnp.minimum(above, line - 1) + y
-
-            @pl.when(below >= 0)
+    def way_copy(way, m, s, j):
+        k = 2 * j + core
+        return pltpu.make_async_remote_copy(
+            src_ref=slot(m, s, k),
+            dst_ref=slot(m, s, k),
+            send_sem=send_sem.at[way, m, s, j],
+            recv_sem=recv_sem.at[m, s, k],
+            device_id=way_ids[way],
+        )
+
+    def cross_copy(m, j):
+        return pltpu.make_async_remote_copy(
+            src_ref=(cross_qkv, cross_out)[m].at[j],
+            dst_ref=slot(m, f, 2 * j + core),
+            send_sem=cross_send.at[m, j],
+            recv_sem=recv_sem.at[m, f, 2 * j + core],
+            device_id=team_ids[1],
+        )
+
+    def arrived(m, s, k):
+        pltpu.make_async_copy(slot(m, s, k), slot(m, s, k), recv_sem.at[m, s, k]).wait()
+
+    def send_both(m, s, j):
+        pl.when(has_up)(way_copy(UP, m, s, j).start)
+        pl.when(has_down)(way_copy(DOWN, m, s, j).start)
+
+    def cross_step(m, j):
+        arrived(m, across, 2 * j + core)
+        send_both(m, across, j)
+        way_copy(PARTNER, m, across, j).start()
+
+    def sides(k, o):
+        row = y if o == 0 else 1 - y
+        below, above = z - k, z + k
+        return (
+            (below >= 0, 2 * jnp.maximum(below, 0) + row, UP, has_up),
+            (above < line, 2 * jnp.minimum(above, line - 1) + row, DOWN, has_down),
+        )
+
+    def line_step(m, k, o, j):
+        for ok, s, way, onward in sides(k, o):
+
+            @pl.when(ok)
             def _():
-                arrived(m, c, s_below)
-
-            send((below >= 0) & has_up, UP, m, c, s_below)
-            if k > 1 or c == 0:
-                send(below >= 0, ACROSS, m, c, s_below)
-            else:
-                send((below >= 0) & even, ACROSS, m, c, s_below)
-
-            @pl.when(above < line)
-            def _():
-                arrived(m, c, s_above)
-
-            send((above < line) & has_down, DOWN, m, c, s_above)
-            if k > 1 or c == 0:
-                send(above < line, ACROSS, m, c, s_above)
-            else:
-                send((above < line) & jnp.logical_not(even), ACROSS, m, c, s_above)
-
-    def half_step(m):
-        arrived(m, 1, across)
-        send(even, UP, m, 1, across)
-        send(jnp.logical_not(even), DOWN, m, 1, across)
-
-    for c in range(2):
-        for copy in locals_[0][c]:
+                arrived(m, s, 2 * j + core)
+                pl.when(onward)(way_copy(way, m, s, j).start)
+                way_copy(PARTNER, m, s, j).start()
+
+    def from_partner(m, s):
+        for j in range(2):
+            arrived(m, s, 2 * j + 1 - core)
+
+    half_rows = seq_rows // 2
+
+    def tok_copy(way, half):
+        source = (0, 0, 1 + half)[way]
+        target = team_ids[way] if way < 2 else team_ids[1 - half]
+        return pltpu.make_async_remote_copy(
+            src_ref=normed.at[pl.ds(source * seq_rows + half * half_rows, half_rows)],
+            dst_ref=normed.at[pl.ds((1 + way) * seq_rows + half * half_rows, half_rows)],
+            send_sem=tok_send.at[way, half],
+            recv_sem=tok_recv.at[way, half],
+            device_id=target,
+        )
+
+    def len_copy(way):
+        return pltpu.make_async_remote_copy(
+            src_ref=len_tile,
+            dst_ref=len_all.at[1 + way],
+            send_sem=len_send.at[way],
+            recv_sem=len_recv.at[way],
+            device_id=team_ids[way],
+        )
+
+    for j in range(2):
+        for copy in own_loads[j]:
             copy.wait()
-        own_line(0, c)
-        send(None, ACROSS, 0, c, f)
-    small = []
-    for peer in peers:
-        for source, dest, ss, rs in (
-            (tokens, tok_all, tok_send, tok_recv),
-            (len_tile, len_all, len_send, len_recv),
-        ):
-            copy = pltpu.make_async_remote_copy(
-                src_ref=source,
-                dst_ref=dest.at[g],
-                send_sem=ss.at[peer],
-                recv_sem=rs.at[g],
-                device_id={"dp": peer},
-            )
-            copy.start()
-            small.append(copy)
-
-    line_step(0, 1)
-    for k in range(2, line - 1):
-        line_step(0, k)
-    half_step(0)
-    for c in range(2):
-        for copy in locals_[1][c]:
+        send_both(0, f, j)
+        for copy in cross_loads[j]:
             copy.wait()
-        own_line(1, c)
+        cross_copy(0, j).start()
 
     tok_local.wait()
     for copy in vectors:
         copy.wait()
-    for peer in peers:
-        pltpu.make_async_copy(tok_all.at[peer], tok_all.at[peer], tok_recv.at[peer]).wait()
-        pltpu.make_async_copy(len_all.at[peer], len_all.at[peer], len_recv.at[peer]).wait()
-
     norm_rows = 16
-    for j in range(groups):
-
-        @pl.loop(0, seq_rows // norm_rows)
+
+    @pl.loop(0, seq_rows // norm_rows)
+    def _(i):
+        at = pl.ds(pl.multiple_of(i * norm_rows, norm_rows), norm_rows)
+        rows = tok_own[at, :].astype(jnp.float32)
+        scale = lax.rsqrt(jnp.mean(rows * rows, axis=-1, keepdims=True) + 1e-06)
+        normed[at, :] = (rows * scale * norm_gain[...]).astype(jnp.bfloat16)
+
+    tok_copy(0, 0).start()
+    tok_copy(1, 1).start()
+    tok_copy(0, 1).start()
+    tok_copy(1, 0).start()
+    for way in range(3):
+        len_copy(way).start()
+
+    bias_parts = (
+        (team * query_cols, query_cols, 0),
+        (QUERY_FEATURES + team * key_cols, key_cols, query_cols),
+        (QUERY_FEATURES + KEY_FEATURES + team * key_cols, key_cols, query_cols + key_cols),
+    )
+    for start, size, to in bias_parts:
+        qkv_rows[:, to : to + size] = jnp.broadcast_to(
+            qkv_bias[:, pl.ds(pl.multiple_of(start, HEAD_SIZE), size)],
+            (groups * seq_rows, size),
+        )
+
+    for j in range(2):
+        cross_step(0, j)
+        line_step(0, 1, 0, j)
+    tok_copy(0, 0).wait_recv()
+    tok_copy(2, 0).start()
+    line_step(0, 1, 1, 0)
+    line_step(0, 1, 1, 1)
+    tok_copy(1, 1).wait_recv()
+    tok_copy(2, 1).start()
+    out_own.wait()
+    for j in range(2):
+        out_cross[j].wait()
+        cross_copy(1, j).start()
+    for k in range(2, line - 1):
+        for o in range(2):
+            for j in range(2):
+                line_step(0, k, o, j)
+    for j in range(2):
+        send_both(1, f, j)
+
+    tok_copy(0, 1).wait_recv()
+    tok_copy(1, 0).wait_recv()
+    tok_copy(2, 0).wait_recv()
+    tok_copy(2, 1).wait_recv()
+    for way in range(3):
+        len_copy(way).wait_recv()
+    for copy in late_loads:
+        copy.wait()
+
+    tile = 3 * HEAD_SIZE
+
+    def qkv_step(place):
+        rows = pl.ds(pl.multiple_of(place * 2 * depth, 128), 2 * depth)
+
+        @pl.loop(0, (query_cols + 2 * key_cols) // tile)
+        def _(t):
+            cols = pl.ds(pl.multiple_of(t * tile, tile), tile)
+            qkv_rows[:, cols] += jnp.dot(
+                normed[:, rows], qkv_full[rows, cols], preferred_element_type=jnp.float32
+            )
+
+    def qkv_places(first, last):
+        @pl.loop(2 * first, 2 * last)
         def _(i):
-            at = pl.multiple_of(i * norm_rows, norm_rows)
-            rows = tok_all[j, pl.ds(at, norm_rows), :].astype(jnp.float32)
-            scale = lax.rsqrt(jnp.mean(rows * rows, axis=-1, keepdims=True) + 1e-06)
-            normed[pl.ds(pl.multiple_of(j * seq_rows + at, norm_rows), norm_rows), :] = (
-                rows * scale * norm_gain[...]
-            ).astype(jnp.bfloat16)
-
-    line_step(0, line - 1)
-    for c in range(2):
-        send(None, ACROSS, 1, c, f)
-
-    def across_wait(m, k):
-        for c in range(2):
-            if k == 0:
-                if c == 0:
-                    arrived(m, c, across)
-                continue
-            for there, ok in ((z - k, z - k >= 0), (z + k, z + k < line)):
-                s = 2 * jnp.clip(there, 0, line - 1) + 1 - y
-
-                @pl.when(ok)
-                def _():
-                    arrived(m, c, s)
-
-    for k in range(line):
-        across_wait(0, k)
-
-    tile = 3 * HEAD_SIZE
-
-    @pl.loop(0, (query_cols + 2 * key_cols) // tile)
-    def _(t):
-        cols = pl.ds(pl.multiple_of(t * tile, tile), tile)
-        qkv_rows[:, cols] = jnp.dot(
-            normed[...], qkv_full[:, cols], preferred_element_type=jnp.float32
-        )
-
-    def head_rows(j, column, bias_at):
-        rows = qkv_rows[pl.ds(pl.multiple_of(j * seq_rows, seq_rows), seq_rows), pl.ds(column, HEAD_SIZE)]
-        return rows + qkv_bias[:, pl.ds(pl.multiple_of(bias_at, HEAD_SIZE), HEAD_SIZE)]
+            k = i // 2
+            place = z + (2 * lax.rem(i, 2) - 1) * k
+
+            @pl.when((place >= 0) & (place < line))
+            def _():
+                from_partner(0, 2 * place)
+                from_partner(0, 2 * place + 1)
+                qkv_step(place)
+
+    @pl.loop(0, 1)
+    def _(i):
+        from_partner(0, across)
+        qkv_step(z)
+
+    qkv_places(1, line - 1)
+    for j in range(2):
+        cross_step(1, j)
+    for o in range(2):
+        for j in range(2):
+            line_step(0, line - 1, o, j)
+    qkv_places(line - 1, line)
+
+    def head_rows(j, column):
+        return qkv_rows[
+            pl.ds(pl.multiple_of(j * seq_rows, seq_rows), seq_rows), column : column + HEAD_SIZE
+        ]
 
     def rotate(rows):
         return (
@@ -378,23 +441,18 @@
     key_heads = key_cols // HEAD_SIZE
     share = heads // key_heads
 
-    def attend_sequence(j):
+    @pl.loop(0, groups)
+    def _(j):
         query_place = lax.broadcasted_iota(jnp.int32, (seq_rows, seq_rows), 0)
         key_place = lax.broadcasted_iota(jnp.int32, (seq_rows, seq_rows), 1)
         allowed = (key_place <= query_place) & (key_place < len_all[j, 0:1, :])
         at = pl.ds(pl.multiple_of(j * seq_rows, seq_rows), seq_rows)
         for kh in range(key_heads):
             offset = kh * HEAD_SIZE
-            key = rotate(
-                head_rows(j, query_cols + offset, QUERY_FEATURES + g * key_cols + offset)
-            )
-            value = head_rows(
-                j,
-                query_cols + key_cols + offset,
-                QUERY_FEATURES + KEY_FEATURES + g * key_cols + offset,
-            ).astype(jnp.bfloat16)
+            key = rotate(head_rows(j, query_cols + offset))
+            value = head_rows(j, query_cols + key_cols + offset).astype(jnp.bfloat16)
             for h in range(kh * share, (kh + 1) * share):
-                query = rotate(head_rows(j, h * HEAD_SIZE, g * query_cols + h * HEAD_SIZE))
+                query = rotate(head_rows(j, h * HEAD_SIZE))
                 scores = lax.dot_general(
                     query, key, (((1,), (1,)), ((), ())), preferred_element_type=jnp.float32
                 ) / np.float32(np.sqrt(HEAD_SIZE))
@@ -405,17 +463,13 @@
                     probs, value, preferred_element_type=jnp.float32
                 ).astype(jnp.bfloat16)
 
-    pl.loop(0, groups // 2)(attend_sequence)
-    line_step(1, 1)
-    pl.loop(groups // 2, groups)(attend_sequence)
-
-    def part_copy(peer, s):
+    def part_copy(way, s):
         return pltpu.make_async_remote_copy(
-            src_ref=part_out.at[s, pl.ds(pl.multiple_of(peer * seq_rows, seq_rows), seq_rows)],
-            dst_ref=part_in.at[g, s],
-            send_sem=part_send.at[peer, s],
-            recv_sem=part_recv.at[g, s],
-            device_id={"dp": peer},
+            src_ref=part_out.at[s, pl.ds((1 + way) * seq_rows, seq_rows)],
+            dst_ref=part_in.at[way, s],
+            send_sem=part_send.at[way, s],
+            recv_sem=part_recv.at[way, s],
+            device_id=team_ids[way],
         )
 
     def project(s):
@@ -426,71 +480,93 @@
             preferred_element_type=jnp.float32,
         )
         part_out[s] = result.astype(jnp.bfloat16)
-        for j in range(groups):
-
-            @pl.when(g == j)
-            def _():
-                own[s] = result[j * seq_rows : (j + 1) * seq_rows]
-
-        for peer in peers:
-            part_copy(peer, s).start()
-
-    def project_places(k, side):
-        @pl.loop(0, 1 if k == 0 else 2)
-        def _(i):
-            there = z + (2 * i - 1) * k
-
-            @pl.when((there >= 0) & (there < line))
-            def _():
-                project(2 * there + side)
-
-    for k in range(2, line - 1):
-        line_step(1, k)
-    half_step(1)
-    across_wait(1, 0)
-
-    @pl.loop(0, 2)
-    def _(side):
-        project(2 * z + side)
-
-    project_places(1, y)
-    line_step(1, line - 1)
-    for k in range(2, line):
-        project_places(k, y)
-    for k in range(1, line):
-        across_wait(1, k)
-        project_places(k, 1 - y)
-
-    @pl.loop(0, shards)
-    def _(s):
-        for peer in peers:
-            pltpu.make_async_copy(
-                part_in.at[peer, s], part_in.at[peer, s], part_recv.at[peer, s]
-            ).wait()
-
-    block = 32
-    out_cols = own.shape[2]
-
-    @pl.loop(0, seq_rows // block)
-    def _(i):
-        at = pl.ds(pl.multiple_of(i * block, block), block)
-        for p in range(shards // 2):
-            sums = []
-            for s in (2 * p, 2 * p + 1):
-                total = own[s, at]
-                for peer in peers:
-                    total += part_in[peer, s, at].astype(jnp.float32)
-                sums.append(total)
-            cols = slice(2 * p * out_cols, 2 * (p + 1) * out_cols)
-            hidden[at, cols] = (
-                tok_all[g, at, cols].astype(jnp.float32) + jnp.concatenate(sums, axis=1)
-            ).astype(jnp.bfloat16)
+        own[s] = result[:seq_rows]
+        for way in (2, 0, 1):
+            part_copy(way, s).start()
 
     place = lax.broadcasted_iota(jnp.int32, len_tile.shape, 1)
     pick = (place == len_tile[...] - 1).astype(jnp.bfloat16)
-    last = jnp.dot(pick, hidden[...], preferred_element_type=jnp.float32)
-    scale = lax.rsqrt(jnp.mean(last * last, axis=-1, keepdims=True) + 1e-06)
-    score = jnp.sum(last * scale * final_gain[...] * value_head[...], axis=-1, keepdims=True)
+    stats[...] = jnp.zeros_like(stats)
+
+    def hidden_copy(place):
+        cols = pl.ds(pl.multiple_of(place * 2 * out_cols, 128), 2 * out_cols)
+        return pltpu.make_async_copy(
+            hidden.at[:, cols], hidden_out.at[:, cols], hidden_sem.at[place]
+        )
+
+    def finish(place):
+        sums = []
+        for s in (2 * place, 2 * place + 1):
+            for way in range(3):
+                part_copy(way, s).wait_recv()
+            total = own[s]
+            for way in range(3):
+                total += part_in[way, s].astype(jnp.float32)
+            sums.append(total)
+        cols = pl.ds(pl.multiple_of(place * 2 * out_cols, 128), 2 * out_cols)
+        hidden[:, cols] = (
+            tok_own[:, cols].astype(jnp.float32) + jnp.concatenate(sums, axis=1)
+        ).astype(jnp.bfloat16)
+        hidden_copy(place).start()
+        last = jnp.dot(pick, hidden[:, cols], preferred_element_type=jnp.float32)
+        weighted = last * final_gain[:, cols] * value_head[:, cols]
+        squares = last * last
+        for t in range(2 * out_cols // HEAD_SIZE):
+            lanes = slice(t * HEAD_SIZE, (t + 1) * HEAD_SIZE)
+            stats[0] += squares[:, lanes]
+            stats[1] += weighted[:, lanes]
+
+    def project_places(k, o):
+        @pl.loop(0, 2)
+        def _(i):
+            place = z + (2 * i - 1) * k
+            s = 2 * place + (y if o == 0 else 1 - y)
+
+            @pl.when((place >= 0) & (place < line))
+            def _():
+                from_partner(1, s)
+                project(s)
+
+    def finish_places(k):
+        @pl.loop(0, 2)
+        def _(i):
+            place = z + (2 * i - 1) * k
+
+            @pl.when((place >= 0) & (place < line))
+            def _():
+                finish(place)
+
+    for j in range(2):
+        line_step(1, 1, 0, j)
+
+    @pl.loop(0, 2)
+    def _(i):
+        @pl.when(i == 1)
+        def _():
+            from_partner(1, across)
+
+        project(jnp.where(i == 0, f, across))
+
+    for k in range(1, line):
+        project_places(k, 0)
+        for j in range(2):
+            line_step(1, k, 1, j)
+        project_places(k, 1)
+        if k < line - 1:
+            for j in range(2):
+                line_step(1, k + 1, 0, j)
+        if k == 1:
+
+            @pl.loop(0, 1)
+            def _(i):
+                finish(z)
+
+        else:
+            finish_places(k - 1)
+    finish_places(line - 1)
+
+    mean = jnp.sum(stats[0], axis=-1, keepdims=True) / width
+    score = jnp.sum(stats[1], axis=-1, keepdims=True) * lax.rsqrt(mean + 1e-06)
     first_row = lax.broadcasted_iota(jnp.int32, score_tile.shape, 0) == 0
     score_tile[...] = jnp.where(first_row, score, jnp.full(score_tile.shape, pair_weight[0]))
     score_all[me] = score_tile[...]
@@ -512,6 +588,36 @@
     @pl.loop(0, everyone)
     def _(i):
         partner_rows[pl.ds(i, 1), :] = jnp.full((1, HEAD_SIZE), partner[i], jnp.int32)
+
+    @pl.loop(0, line)
+    def _(place):
+        hidden_copy(place).wait()
+
+    for m in range(2):
+        for j in range(2):
+            cross_copy(m, j).wait_send()
+
+    @pl.loop(0, shards)
+    def _(s):
+        for way, ok in (
+            (UP, has_up & (s // 2 <= z)),
+            (DOWN, has_down & (s // 2 >= z)),
+            (PARTNER, s != f),
+        ):
+
+            @pl.when(ok)
+            def _():
+                for m in range(2):
+                    for j in range(2):
+                        way_copy(way, m, s, j).wait_send()
+
+        for way in range(3):
+            part_copy(way, s).wait_send()
+
+    for way in range(3):
+        len_copy(way).wait_send()
+        for half in range(2):
+            tok_copy(way, half).wait_send()
 
     @pl.loop(1, everyone)
     def _(i):
@@ -533,19 +639,6 @@
     margin_out[0] = jnp.sum(jnp.where(first_lane & (row == me), margins, 0.0))
     loss_out[0] = jnp.sum(jnp.where(first_lane, weights * softplus, 0.0)) / everyone
 
-    for cond, copy in started:
-        if cond is None:
-            copy.wait_send()
-        else:
-            pl.when(cond)(copy.wait_send)
-    for copy in small:
-        copy.wait_send()
-
-    @pl.loop(0, shards)
-    def _(s):
-        for peer in peers:
-            part_copy(peer, s).wait_send()
-
     @pl.loop(1, everyone)
     def _(i):
         score_copy(i).wait_send()
@@ -553,12 +646,12 @@
 
 def layer_fits(shards, groups, tokens, qkv_weight, out_weight):
     return (
-        shards % 4 == 0
+        shards % 2 == 0
         and shards >= 8
-        and qkv_weight.shape[0] % 32 == 0
+        and qkv_weight.shape[0] % 64 == 0
+        and groups == 4
         and KEY_VALUE_HEADS % groups == 0
         and tokens.shape[1] == HEAD_SIZE
-        and groups % 2 == 0
         and shards * groups <= HEAD_SIZE
         and out_weight.shape[1] % 64 == 0
     )
@@ -599,11 +692,13 @@
             jax.ShapeDtypeStruct((1,), f32),
         ),
         in_specs=[anywhere] * 3 + [scalar] * 3 + [anywhere] * 4 + [vmem] * 2,
-        out_specs=(vmem, scalar, scalar),
+        out_specs=(anywhere, scalar, scalar),
         scratch_shapes=[
             pltpu.VMEM((shards * depth, all_cols), bf16),
             pltpu.VMEM((shards, out_cols, query_cols), bf16),
-            pltpu.VMEM((groups, seq_rows, width), bf16),
+            pltpu.VMEM((2, depth // 4, all_cols), bf16),
+            pltpu.VMEM((2, out_cols // 4, query_cols), bf16),
+            pltpu.VMEM((seq_rows, width), bf16),
             pltpu.VMEM((8, seq_rows), jnp.int32),
             pltpu.VMEM((groups, 8, seq_rows), jnp.int32),
             pltpu.VMEM((rows, width), bf16),
@@ -611,25 +706,29 @@
             pltpu.VMEM((rows, query_cols), bf16),
             pltpu.VMEM((shards, seq_rows, out_cols), f32),
             pltpu.VMEM((shards, rows, out_cols), bf16),
-            pltpu.VMEM((groups, shards, seq_rows, out_cols), bf16),
+            pltpu.VMEM((groups - 1, shards, seq_rows, out_cols), bf16),
+            pltpu.VMEM((seq_rows, width), bf16),
+            pltpu.VMEM((2, 8, HEAD_SIZE), f32),
             pltpu.VMEM((8, HEAD_SIZE), f32),
             pltpu.VMEM((everyone, 8, HEAD_SIZE), f32),
             pltpu.VMEM((everyone, HEAD_SIZE), jnp.int32),
             pltpu.VMEM((1, width), f32),
-            pltpu.VMEM((1, width), f32),
-            pltpu.VMEM((1, width), f32),
-            pltpu.VMEM((1, qkv_bias.shape[0]), f32),
-            dma((13,)),
-            dma((2, 2, shards)),
-            dma((3, 2, 2, shards)),
-            dma((groups,)),
-            dma((groups,)),
-            dma((groups,)),
-            dma((groups,)),
-            dma((groups, shards)),
-            dma((groups, shards)),
+            pltpu.VMEM((1, width + 8 * HEAD_SIZE), f32),
+            pltpu.VMEM((1, width + 8 * HEAD_SIZE), f32),
+            pltpu.VMEM((1, qkv_bias.shape[0] + 8 * HEAD_SIZE), f32),
+            dma((26,)),
+            dma((2, shards, 4)),
+            dma((3, 2, shards, 2)),
+            dma((2, 2)),
+            dma((3, 2)),
+            dma((3, 2)),
+            dma((3,)),
+            dma((3,)),
+            dma((3, shards)),
+            dma((3, shards)),
             dma((everyone,)),
             dma((everyone,)),
+            dma((shards // 2,)),
         ],
         compiler_params=pltpu.CompilerParams(
             collective_id=0, has_side_effects=True, vmem_limit_bytes=60 * 1024 * 1024

time: 186 us -> 154 us (0.83)
  Pallas kernels: 178 us -> 146 us
    pallas_call x1, Pallas kernels: 178 us -> 146 us  [layer(): pl.pallas_call(functools.partial(layer_kernel, shards, groups), out_shape...]
where the time goes in v1:
time: 154 us
  Pallas kernels  146 us (95%)
  between operations  5.48 us (4%)
  local copies, waits for them, and re-layouts  2.16 us (1%)
    pallas_call x1, Pallas kernels, layer(): pl.pallas_call(functools.partial(layer_kernel, shards, groups), out_shape...  146 us

profile of v1, /device:TPU:0, one launch (start us, length us, event | category | flops | bytes accessed | tf_op | source)
XLA Modules:
  0.0 153.6 jit_solution(878999334556497683)
XLA Ops:
  1.9 146.0 %shard_map.139 = (bf16[128,3584]{1,0:T(8,128)(2,1)}, f32[1]{0:T(128)}, f32[1]{0:T(128)}) custom-call(bf16[128,3584]{1,0:T(8,128)(2,1)} %bitcast.5, bf16[448,4608]{1,0:T(8,128)(2,1)} %qkv_weight.1, bf16[448,3584]{1,0:T(8,128)(2,1)} %bitcast.4, s32[1]{0:T(128)S(6)} %copy.18.length, f32[1]{0:T(128)S(6)} %copy.19.pair_weight, s32[32]{0:T(128)} %partner.1, ...), custom_call_target="tpu_custom_call" | custom-call | tf_op jit(solution)/shard_map/pallas_call | solution.py:687
  147.9 2.2 %copy.20 = bf16[1,128,3584]{2,1,0:T(8,128)(2,1)} copy(bf16[1,128,3584]{2,1,0:T(8,128)(2,1)} %bitcast.6) | data formatting | bytes 1835008

commit v2 on v1

--- a/solution.py
+++ b/solution.py
@@ -101,16 +101,16 @@
     tokens,
     qkv_weight,
     out_weight,
-    length,
-    pair_weight,
-    partner,
+    length_one,
+    pair_weight_one,
+    partner_all,
     norm_gain_flat,
     final_gain_flat,
     value_head_flat,
     qkv_bias_flat,
-    cosine,
-    sine,
-    hidden_out,
+    cosine_table,
+    sine_table,
+    hidden,
     margin_out,
     loss_out,
     qkv_full,
@@ -126,7 +126,6 @@
     own,
     part_out,
     part_in,
-    hidden,
     stats,
     score_tile,
     score_all,
@@ -135,6 +134,11 @@
     final_gain,
     value_head,
     qkv_bias,
+    cosine,
+    sine,
+    length,
+    pair_weight,
+    partner,
     local_sem,
     recv_sem,
     send_sem,
@@ -147,7 +151,6 @@
     part_recv,
     score_send,
     score_recv,
-    hidden_sem,
 ):
     line = shards // 2
     f = lax.axis_index("fsdp")
@@ -174,6 +177,15 @@
     team_ids = ({"dp": x_peer}, {"fsdp": across}, {"fsdp": across, "dp": x_peer})
     way_ids = ({"fsdp": f + 2}, {"fsdp": f - 2}, {"dp": 2 * x + 1 - core})
 
+    barrier = pltpu.get_barrier_semaphore()
+    for target in (*team_ids, way_ids[PARTNER]):
+        pl.semaphore_signal(barrier, inc=1, device_id=target)
+    for way, ok in ((UP, has_up), (DOWN, has_down)):
+
+        @pl.when(ok)
+        def _():
+            pl.semaphore_signal(barrier, inc=1, device_id=way_ids[way])
+
     def slot(m, s, k):
         if m == 0:
             return qkv_full.at[pl.ds(pl.multiple_of(s * depth + k * quarter, 16), quarter)]
@@ -202,6 +214,7 @@
             )
         ]
 
+    length_load = local(length_one, length)
     own_loads, cross_loads = [], []
     for j in range(2):
         k = 2 * j + core
@@ -234,21 +247,19 @@
         )
         for j in range(2)
     ]
-    len_tile[...] = jnp.full(len_tile.shape, length[0], jnp.int32)
-    len_all[0] = len_tile[...]
-
-    barrier = pltpu.get_barrier_semaphore()
+    small_loads = [
+        local(source, dest)
+        for source, dest in (
+            (pair_weight_one, pair_weight),
+            (partner_all, partner),
+            (cosine_table, cosine),
+            (sine_table, sine),
+        )
+    ]
     everyone = shards * groups
     me = f * groups + g
 
-    @pl.loop(1, everyone)
-    def _(i):
-        other = lax.rem(me + i, everyone)
-        pl.semaphore_signal(
-            barrier, inc=1, device_id={"fsdp": other // groups, "dp": lax.rem(other, groups)}
-        )
-
-    pl.semaphore_wait(barrier, everyone - 1)
+    pl.semaphore_wait(barrier, 4 + has_up.astype(jnp.int32) + has_down.astype(jnp.int32))
 
     def way_copy(way, m, s, j):
         k = 2 * j + core
@@ -348,6 +359,9 @@
     tok_copy(1, 1).start()
     tok_copy(0, 1).start()
     tok_copy(1, 0).start()
+    length_load.wait()
+    len_tile[...] = jnp.full(len_tile.shape, length[0], jnp.int32)
+    len_all[0] = len_tile[...]
     for way in range(3):
         len_copy(way).start()
 
@@ -388,8 +402,12 @@
     tok_copy(2, 1).wait_recv()
     for way in range(3):
         len_copy(way).wait_recv()
-    for copy in late_loads:
+    for copy in (*late_loads, *small_loads):
         copy.wait()
+
+    @pl.loop(0, everyone)
+    def _(i):
+        partner_rows[pl.ds(i, 1), :] = jnp.full((1, HEAD_SIZE), partner[i], jnp.int32)
 
     tile = 3 * HEAD_SIZE
 
@@ -488,12 +506,6 @@
     pick = (place == len_tile[...] - 1).astype(jnp.bfloat16)
     stats[...] = jnp.zeros_like(stats)
 
-    def hidden_copy(place):
-        cols = pl.ds(pl.multiple_of(place * 2 * out_cols, 128), 2 * out_cols)
-        return pltpu.make_async_copy(
-            hidden.at[:, cols], hidden_out.at[:, cols], hidden_sem.at[place]
-        )
-
     def finish(place):
         sums = []
         for s in (2 * place, 2 * place + 1):
@@ -507,7 +519,6 @@
         hidden[:, cols] = (
             tok_own[:, cols].astype(jnp.float32) + jnp.concatenate(sums, axis=1)
         ).astype(jnp.bfloat16)
-        hidden_copy(place).start()
         last = jnp.dot(pick, hidden[:, cols], preferred_element_type=jnp.float32)
         weighted = last * final_gain[:, cols] * value_head[:, cols]
         squares = last * last
@@ -584,14 +595,6 @@
     @pl.loop(1, everyone)
     def _(i):
         score_copy(i).start()
-
-    @pl.loop(0, everyone)
-    def _(i):
-        partner_rows[pl.ds(i, 1), :] = jnp.full((1, HEAD_SIZE), partner[i], jnp.int32)
-
-    @pl.loop(0, line)
-    def _(place):
-        hidden_copy(place).wait()
 
     for m in range(2):
         for j in range(2):
@@ -636,8 +639,10 @@
     margins = jnp.where(row < partners, scores - others, others - scores)
     softplus = jnp.maximum(-margins, 0.0) + jnp.log1p(jnp.exp(-jnp.abs(margins)))
     first_lane = lane == 0
-    margin_out[0] = jnp.sum(jnp.where(first_lane & (row == me), margins, 0.0))
-    loss_out[0] = jnp.sum(jnp.where(first_lane, weights * softplus, 0.0)) / everyone
+    margin = jnp.sum(jnp.where(first_lane & (row == me), margins, 0.0))
+    loss = jnp.sum(jnp.where(first_lane, weights * softplus, 0.0)) / everyone
+    margin_out[0] = margin
+    loss_out[0] = loss
 
     @pl.loop(1, everyone)
     def _(i):
@@ -681,18 +686,17 @@
     everyone = shards * groups
     dma = pltpu.SemaphoreType.DMA
     vmem = pl.BlockSpec(memory_space=pltpu.VMEM)
-    anywhere = pl.BlockSpec(memory_space=pl.ANY)
+    scalar = pl.BlockSpec(memory_space=pltpu.SMEM)
     bf16, f32 = jnp.bfloat16, jnp.float32
-    scalar = pl.BlockSpec(memory_space=pltpu.SMEM)
     hidden, margin, loss = pl.pallas_call(
         functools.partial(layer_kernel, shards, groups),
         out_shape=(
-            jax.ShapeDtypeStruct((seq_rows, width), bf16),
-            jax.ShapeDtypeStruct((1,), f32),
-            jax.ShapeDtypeStruct((1,), f32),
+            pltpu.VMEM((seq_rows, width), bf16),
+            pltpu.SMEM((1,), f32),
+            pltpu.SMEM((1,), f32),
         ),
-        in_specs=[anywhere] * 3 + [scalar] * 3 + [anywhere] * 4 + [vmem] * 2,
-        out_specs=(anywhere, scalar, scalar),
+        in_specs=[pl.BlockSpec(memory_space=pltpu.HBM)] * 12,
+        out_specs=(vmem, scalar, scalar),
         scratch_shapes=[
             pltpu.VMEM((shards * depth, all_cols), bf16),
             pltpu.VMEM((shards, out_cols, query_cols), bf16),
@@ -707,7 +711,6 @@
             pltpu.VMEM((shards, seq_rows, out_cols), f32),
             pltpu.VMEM((shards, rows, out_cols), bf16),
             pltpu.VMEM((groups - 1, shards, seq_rows, out_cols), bf16),
-            pltpu.VMEM((seq_rows, width), bf16),
             pltpu.VMEM((2, 8, HEAD_SIZE), f32),
             pltpu.VMEM((8, HEAD_SIZE), f32),
             pltpu.VMEM((everyone, 8, HEAD_SIZE), f32),
@@ -716,7 +719,12 @@
             pltpu.VMEM((1, width + 8 * HEAD_SIZE), f32),
             pltpu.VMEM((1, width + 8 * HEAD_SIZE), f32),
             pltpu.VMEM((1, qkv_bias.shape[0] + 8 * HEAD_SIZE), f32),
-            dma((26,)),
+            pltpu.VMEM((seq_rows, HEAD_SIZE), f32),
+            pltpu.VMEM((seq_rows, HEAD_SIZE), f32),
+            pltpu.SMEM((1,), jnp.int32),
+            pltpu.SMEM((1,), f32),
+            pltpu.SMEM((everyone,), jnp.int32),
+            dma((31,)),
             dma((2, shards, 4)),
             dma((3, 2, shards, 2)),
             dma((2, 2)),
@@ -728,10 +736,9 @@
             dma((3, shards)),
             dma((everyone,)),
             dma((everyone,)),
-            dma((shards // 2,)),
         ],
         compiler_params=pltpu.CompilerParams(
-            collective_id=0, has_side_effects=True, vmem_limit_bytes=60 * 1024 * 1024
+            collective_id=0, has_side_effects=True, vmem_limit_bytes=56 * 1024 * 1024
         ),
     )(
         tokens[0],

time: 154 us -> 147 us (0.955)
  Pallas kernels: 146 us -> 143 us
  between operations: 5.48 us -> 2.97 us
    pallas_call x1, Pallas kernels: 146 us -> 143 us  [layer(): pl.pallas_call(functools.partial(layer_kernel, shards, groups), out_shape...]
where the time goes in v2:
time: 147 us
  Pallas kernels  143 us (97%)
  between operations  2.97 us (2%)
    pallas_call x1, Pallas kernels, layer(): pl.pallas_call(functools.partial(layer_kernel, shards, groups), out_shape...  143 us

profile of v2, /device:TPU:0, one launch (start us, length us, event | category | flops | bytes accessed | tf_op | source)
XLA Modules:
  0.0 147.0 jit_solution(14031779902499984022)
XLA Ops:
  1.9 143.1 %shard_map.139 = (bf16[128,3584]{1,0:T(8,128)(2,1)S(1)}, f32[1]{0:T(128)S(4)}, f32[1]{0:T(128)S(4)}) custom-call(bf16[128,3584]{1,0:T(8,128)(2,1)} %bitcast.6, bf16[448,4608]{1,0:T(8,128)(2,1)} %qkv_weight.1, bf16[448,3584]{1,0:T(8,128)(2,1)} %bitcast.5, s32[1]{0:T(128)S(6)} %copy.21.length_one, f32[1]{0:T(128)S(6)} %copy.22.pair_weight_one, s32[32]{0:T(128)} %partner_all.1, ...), custom_call_target="tpu_custom_call" | custom-call | tf_op jit(solution)/shard_map/pallas_call | solution.py:691
  146.0 0.9 copy.18

commit v3 on v2

--- a/solution.py
+++ b/solution.py
@@ -93,6 +93,11 @@
         np.concatenate([cosine, cosine], axis=1).astype(np.float32),
         np.concatenate([-sine, sine], axis=1).astype(np.float32),
     )
+
+
+def out_pieces(out_cols):
+    big = (out_cols // 2 + HEAD_SIZE - 1) // HEAD_SIZE * HEAD_SIZE
+    return big, out_cols - big
 
 
 def layer_kernel(
@@ -126,6 +131,12 @@
     own,
     part_out,
     part_in,
+    attn_help,
+    help_own,
+    help_out,
+    help_in,
+    help_sum,
+    help_done,
     stats,
     score_tile,
     score_all,
@@ -149,6 +160,11 @@
     len_recv,
     part_send,
     part_recv,
+    attn_send,
+    attn_recv,
+    help_send,
+    help_recv,
+    done_sem,
     score_send,
     score_recv,
 ):
@@ -167,7 +183,13 @@
     key_cols = KEY_FEATURES // groups
     heads = query_cols // HEAD_SIZE
     quarter = depth // 4
-    out_quarter = out_cols // 4
+    pair = 2 * out_cols
+    big, small = out_pieces(out_cols)
+    is_end = (z == 0) | (z == line - 1)
+    is_helper = (z == 1) | (z == line - 2)
+    far = jnp.where((z == 0) | (z == 1), line - 1, 0)
+    end_to_helper = {"fsdp": jnp.where(z == 0, f + 2, f - 2)}
+    helper_to_end = {"fsdp": jnp.where(z == 1, f - 2, f + 2)}
     has_up = z < line - 1
     has_down = z > 0
     team = 2 * x + y
@@ -186,10 +208,17 @@
         def _():
             pl.semaphore_signal(barrier, inc=1, device_id=way_ids[way])
 
-    def slot(m, s, k):
+    def out_rows(side, piece, half):
+        size = (big, small)[piece] // 2
+        start = (side * small, (1 - side) * big)[piece]
+        return start + half * size, size
+
+    def slot(m, s, piece, half):
         if m == 0:
-            return qkv_full.at[pl.ds(pl.multiple_of(s * depth + k * quarter, 16), quarter)]
-        return out_full.at[s, pl.ds(pl.multiple_of(k * out_quarter, 16), out_quarter)]
+            start = s * depth + (2 * piece + half) * quarter
+            return qkv_full.at[pl.ds(pl.multiple_of(start, 16), quarter)]
+        start, size = out_rows(lax.rem(s, 2), piece, half)
+        return out_full.at[pl.ds(pl.multiple_of(s * out_cols + start, 16), size)]
 
     count = 0
 
@@ -200,8 +229,8 @@
         copy.start()
         return copy
 
-    def qkv_parts(k, owner, dest):
-        rows = pl.ds(pl.multiple_of(k * quarter, 16), quarter)
+    def qkv_parts(piece, half, owner, dest):
+        rows = pl.ds(pl.multiple_of((2 * piece + half) * quarter, 16), quarter)
         return [
             local(
                 qkv_weight.at[rows, pl.ds(pl.multiple_of(start, 128), size)],
@@ -217,9 +246,8 @@
     length_load = local(length_one, length)
     own_loads, cross_loads = [], []
     for j in range(2):
-        k = 2 * j + core
-        own_loads.append(qkv_parts(k, team, slot(0, f, k)))
-        cross_loads.append(qkv_parts(k, across_team, cross_qkv.at[j]))
+        own_loads.append(qkv_parts(j, core, team, slot(0, f, j, core)))
+        cross_loads.append(qkv_parts(j, core, across_team, cross_qkv.at[j]))
     tok_local = local(tokens, tok_own)
     vectors = [
         local(flat, row.at[0, pl.ds(0, flat.shape[0])])
@@ -232,21 +260,29 @@
     ]
     late_loads = []
     for j in range(2):
-        k = 2 * j + 1 - core
-        late_loads.extend(qkv_parts(k, team, slot(0, f, k)))
+        late_loads.extend(qkv_parts(j, 1 - core, team, slot(0, f, j, 1 - core)))
     out_own = local(
-        out_weight.at[:, pl.ds(pl.multiple_of(team * query_cols, 128), query_cols)], out_full.at[f]
-    )
-    out_cross = [
-        local(
-            out_weight.at[
-                pl.ds(pl.multiple_of((2 * j + core) * out_quarter, 16), out_quarter),
-                pl.ds(pl.multiple_of(across_team * query_cols, 128), query_cols),
-            ],
-            cross_out.at[j],
-        )
-        for j in range(2)
-    ]
+        out_weight.at[:, pl.ds(pl.multiple_of(team * query_cols, 128), query_cols)],
+        out_full.at[pl.ds(pl.multiple_of(f * out_cols, 16), out_cols)],
+    )
+
+    def cross_part(m, j):
+        if m == 0:
+            return cross_qkv.at[j]
+        return cross_out.at[j, pl.ds(0, (small, big)[j] // 2)]
+
+    out_cross = []
+    for j in range(2):
+        start, size = out_rows(y, 1 - j, core)
+        out_cross.append(
+            local(
+                out_weight.at[
+                    pl.ds(pl.multiple_of(start, 16), size),
+                    pl.ds(pl.multiple_of(across_team * query_cols, 128), query_cols),
+                ],
+                cross_part(1, j),
+            )
+        )
     small_loads = [
         local(source, dest)
         for source, dest in (
@@ -261,36 +297,41 @@
 
     pl.semaphore_wait(barrier, 4 + has_up.astype(jnp.int32) + has_down.astype(jnp.int32))
 
-    def way_copy(way, m, s, j):
-        k = 2 * j + core
+    def way_copy(way, m, s, piece):
         return pltpu.make_async_remote_copy(
-            src_ref=slot(m, s, k),
-            dst_ref=slot(m, s, k),
-            send_sem=send_sem.at[way, m, s, j],
-            recv_sem=recv_sem.at[m, s, k],
+            src_ref=slot(m, s, piece, core),
+            dst_ref=slot(m, s, piece, core),
+            send_sem=send_sem.at[way, m, s, piece],
+            recv_sem=recv_sem.at[m, s, piece, core],
             device_id=way_ids[way],
         )
 
+    def piece_of(m, o, j):
+        return 1 - j if m == 1 and o == 1 else j
+
     def cross_copy(m, j):
+        piece = piece_of(m, 1, j)
         return pltpu.make_async_remote_copy(
-            src_ref=(cross_qkv, cross_out)[m].at[j],
-            dst_ref=slot(m, f, 2 * j + core),
+            src_ref=cross_part(m, j),
+            dst_ref=slot(m, f, piece, core),
             send_sem=cross_send.at[m, j],
-            recv_sem=recv_sem.at[m, f, 2 * j + core],
+            recv_sem=recv_sem.at[m, f, piece, core],
             device_id=team_ids[1],
         )
 
-    def arrived(m, s, k):
-        pltpu.make_async_copy(slot(m, s, k), slot(m, s, k), recv_sem.at[m, s, k]).wait()
-
-    def send_both(m, s, j):
-        pl.when(has_up)(way_copy(UP, m, s, j).start)
-        pl.when(has_down)(way_copy(DOWN, m, s, j).start)
+    def arrived(m, s, piece, half):
+        there = slot(m, s, piece, half)
+        pltpu.make_async_copy(there, there, recv_sem.at[m, s, piece, half]).wait()
+
+    def send_both(m, s, piece):
+        pl.when(has_up)(way_copy(UP, m, s, piece).start)
+        pl.when(has_down)(way_copy(DOWN, m, s, piece).start)
 
     def cross_step(m, j):
-        arrived(m, across, 2 * j + core)
-        send_both(m, across, j)
-        way_copy(PARTNER, m, across, j).start()
+        piece = piece_of(m, 1, j)
+        arrived(m, across, piece, core)
+        send_both(m, across, piece)
+        way_copy(PARTNER, m, across, piece).start()
 
     def sides(k, o):
         row = y if o == 0 else 1 - y
@@ -301,17 +342,20 @@
         )
 
     def line_step(m, k, o, j):
+        piece = piece_of(m, o, j)
         for ok, s, way, onward in sides(k, o):
+            if m == 1:
+                onward = onward & (k < line - 2)
 
             @pl.when(ok)
             def _():
-                arrived(m, s, 2 * j + core)
-                pl.when(onward)(way_copy(way, m, s, j).start)
-                way_copy(PARTNER, m, s, j).start()
+                arrived(m, s, piece, core)
+                pl.when(onward)(way_copy(way, m, s, piece).start)
+                way_copy(PARTNER, m, s, piece).start()
 
     def from_partner(m, s):
-        for j in range(2):
-            arrived(m, s, 2 * j + 1 - core)
+        for piece in range(2):
+            arrived(m, s, piece, 1 - core)
 
     half_rows = seq_rows // 2
 
@@ -459,8 +503,19 @@
     key_heads = key_cols // HEAD_SIZE
     share = heads // key_heads
 
+    def attn_copy(j):
+        rows = pl.ds(pl.multiple_of(j * seq_rows, seq_rows), seq_rows)
+        return pltpu.make_async_remote_copy(
+            src_ref=attn.at[rows],
+            dst_ref=attn_help.at[rows],
+            send_sem=attn_send.at[j],
+            recv_sem=attn_recv.at[j],
+            device_id=end_to_helper,
+        )
+
     @pl.loop(0, groups)
-    def _(j):
+    def _(i):
+        j = groups - 1 - i
         query_place = lax.broadcasted_iota(jnp.int32, (seq_rows, seq_rows), 0)
         key_place = lax.broadcasted_iota(jnp.int32, (seq_rows, seq_rows), 1)
         allowed = (key_place <= query_place) & (key_place < len_all[j, 0:1, :])
@@ -480,101 +535,179 @@
                 attn[at, h * HEAD_SIZE : (h + 1) * HEAD_SIZE] = jnp.dot(
                     probs, value, preferred_element_type=jnp.float32
                 ).astype(jnp.bfloat16)
-
-    def part_copy(way, s):
+        pl.when(is_end)(attn_copy(j).start)
+
+    def lanes_of(at, size):
+        return pl.ds(pl.multiple_of(at, HEAD_SIZE), size)
+
+    units = ((0, big), (big, 2 * small), (pair - big, big))
+
+    def part_copy(way, place, at, size, unit):
+        cols = lanes_of(at, size)
         return pltpu.make_async_remote_copy(
-            src_ref=part_out.at[s, pl.ds((1 + way) * seq_rows, seq_rows)],
-            dst_ref=part_in.at[way, s],
-            send_sem=part_send.at[way, s],
-            recv_sem=part_recv.at[way, s],
+            src_ref=part_out.at[place, pl.ds((1 + way) * seq_rows, seq_rows), cols],
+            dst_ref=part_in.at[way, place, :, cols],
+            send_sem=part_send.at[way, place, unit],
+            recv_sem=part_recv.at[way, place, unit],
             device_id=team_ids[way],
         )
 
-    def project(s):
+    def project(place, at, size, unit):
+        cols = lanes_of(at, size)
         result = lax.dot_general(
             attn[...],
-            out_full[s],
+            out_full[lanes_of(place * pair + at, size), :],
             (((1,), (1,)), ((), ())),
             preferred_element_type=jnp.float32,
         )
-        part_out[s] = result.astype(jnp.bfloat16)
-        own[s] = result[:seq_rows]
+        part_out[place, :, cols] = result.astype(jnp.bfloat16)
+        own[place, :, cols] = result[:seq_rows]
         for way in (2, 0, 1):
-            part_copy(way, s).start()
+            part_copy(way, place, at, size, unit).start()
+
+    def project_pair(place):
+        @pl.loop(0, 2)
+        def _(i):
+            project(place, i * (pair - big), big, 2 * i)
+
+        project(place, big, 2 * small, 1)
 
     place = lax.broadcasted_iota(jnp.int32, len_tile.shape, 1)
     pick = (place == len_tile[...] - 1).astype(jnp.bfloat16)
     stats[...] = jnp.zeros_like(stats)
 
-    def finish(place):
-        sums = []
-        for s in (2 * place, 2 * place + 1):
-            for way in range(3):
-                part_copy(way, s).wait_recv()
-            total = own[s]
-            for way in range(3):
-                total += part_in[way, s].astype(jnp.float32)
-            sums.append(total)
-        cols = pl.ds(pl.multiple_of(place * 2 * out_cols, 128), 2 * out_cols)
-        hidden[:, cols] = (
-            tok_own[:, cols].astype(jnp.float32) + jnp.concatenate(sums, axis=1)
-        ).astype(jnp.bfloat16)
+    def finish(place, sums):
+        cols = lanes_of(place * pair, pair)
+        hidden[:, cols] = (tok_own[:, cols].astype(jnp.float32) + sums).astype(jnp.bfloat16)
         last = jnp.dot(pick, hidden[:, cols], preferred_element_type=jnp.float32)
         weighted = last * final_gain[:, cols] * value_head[:, cols]
         squares = last * last
-        for t in range(2 * out_cols // HEAD_SIZE):
+        for t in range(pair // HEAD_SIZE):
             lanes = slice(t * HEAD_SIZE, (t + 1) * HEAD_SIZE)
             stats[0] += squares[:, lanes]
             stats[1] += weighted[:, lanes]
 
-    def project_places(k, o):
+    def finish_parts(place):
+        for unit, (at, size) in enumerate(units):
+            for way in range(3):
+                part_copy(way, place, at, size, unit).wait_recv()
+        total = own[place]
+        for way in range(3):
+            total += part_in[way, place].astype(jnp.float32)
+        finish(place, total)
+
+    def at_sides(k, body):
         @pl.loop(0, 2)
         def _(i):
             place = z + (2 * i - 1) * k
-            s = 2 * place + (y if o == 0 else 1 - y)
-
-            @pl.when((place >= 0) & (place < line))
+
+            @pl.when((place >= 0) & (place < line) & ((k > 0) | (i == 0)))
             def _():
-                from_partner(1, s)
-                project(s)
-
-    def finish_places(k):
-        @pl.loop(0, 2)
+                body(place)
+
+    def own_unit(place):
+        arrived(1, 2 * place + y, 0, 1 - core)
+        project(place, y * (pair - big), big, 2 * y)
+
+    def mid_unit(place):
+        arrived(1, 2 * place + y, 1, 1 - core)
+        arrived(1, 2 * place + 1 - y, 1, 1 - core)
+        project(place, big, 2 * small, 1)
+
+    def cross_unit(place):
+        arrived(1, 2 * place + 1 - y, 0, 1 - core)
+        project(place, (1 - y) * (pair - big), big, 2 * (1 - y))
+
+    from_partner(1, across)
+    project_pair(z)
+
+    @pl.loop(1, line - 1)
+    def _(k):
+        mine = jnp.logical_not(is_helper) | (k < line - 2)
+        line_step(1, k, 0, 0)
+        line_step(1, k, 0, 1)
+
+        @pl.when(mine)
+        def _():
+            at_sides(k, own_unit)
+
+        @pl.when(jnp.logical_not(is_helper))
+        def _():
+            at_sides(k - 1, finish_parts)
+
+        line_step(1, k, 1, 0)
+
+        @pl.when(mine)
+        def _():
+            at_sides(k, mid_unit)
+
+        line_step(1, k, 1, 1)
+
+        @pl.when(mine)
+        def _():
+            at_sides(k, cross_unit)
+
+    def help_part(way):
+        return pltpu.make_async_remote_copy(
+            src_ref=help_out.at[1 + way],
+            dst_ref=help_in.at[way],
+            send_sem=help_send.at[way],
+            recv_sem=help_recv.at[way],
+            device_id=team_ids[way],
+        )
+
+    done_copy = pltpu.make_async_remote_copy(
+        src_ref=help_sum,
+        dst_ref=help_done,
+        send_sem=done_sem.at[0],
+        recv_sem=done_sem.at[1],
+        device_id=helper_to_end,
+    )
+
+    @pl.when(is_helper)
+    def _():
+        for o in range(2):
+            from_partner(1, 2 * far + o)
+
+        @pl.loop(0, groups)
         def _(i):
-            place = z + (2 * i - 1) * k
-
-            @pl.when((place >= 0) & (place < line))
-            def _():
-                finish(place)
-
-    for j in range(2):
-        line_step(1, 1, 0, j)
-
-    @pl.loop(0, 2)
-    def _(i):
-        @pl.when(i == 1)
-        def _():
-            from_partner(1, across)
-
-        project(jnp.where(i == 0, f, across))
-
-    for k in range(1, line):
-        project_places(k, 0)
-        for j in range(2):
-            line_step(1, k, 1, j)
-        project_places(k, 1)
-        if k < line - 1:
-            for j in range(2):
-                line_step(1, k + 1, 0, j)
-        if k == 1:
-
-            @pl.loop(0, 1)
-            def _(i):
-                finish(z)
-
-        else:
-            finish_places(k - 1)
-    finish_places(line - 1)
+            j = groups - 1 - i
+            rows = pl.ds(pl.multiple_of(j * seq_rows, seq_rows), seq_rows)
+            pltpu.make_async_copy(attn_help.at[rows], attn_help.at[rows], attn_recv.at[j]).wait()
+            result = lax.dot_general(
+                attn_help[rows, :],
+                out_full[lanes_of(far * pair, pair), :],
+                (((1,), (1,)), ((), ())),
+                preferred_element_type=jnp.float32,
+            )
+            help_own[...] = result
+            help_out[j] = result.astype(jnp.bfloat16)
+            for way in range(3):
+                pl.when(j == way + 1)(help_part(way).start)
+
+        project_pair(far)
+
+        @pl.loop(0, line)
+        def _(place):
+            pl.when(place != far)(lambda: finish_parts(place))
+
+        for way in range(3):
+            help_part(way).wait_recv()
+        total = help_own[...]
+        for way in range(3):
+            total += help_in[way].astype(jnp.float32)
+        help_sum[...] = total.astype(jnp.bfloat16)
+        done_copy.start()
+
+    @pl.when(is_end)
+    def _():
+        at_sides(line - 2, finish_parts)
+        done_copy.wait_recv()
+        finish(far, help_done[...].astype(jnp.float32))
+
+    @pl.when(is_helper)
+    def _():
+        finish_parts(far)
 
     mean = jnp.sum(stats[0], axis=-1, keepdims=True) / width
     score = jnp.sum(stats[1], axis=-1, keepdims=True) * lax.rsqrt(mean + 1e-06)
@@ -602,20 +735,39 @@
 
     @pl.loop(0, shards)
     def _(s):
-        for way, ok in (
-            (UP, has_up & (s // 2 <= z)),
-            (DOWN, has_down & (s // 2 >= z)),
-            (PARTNER, s != f),
+        place = s // 2
+        skipped = (place == far) & is_end
+        for way, ok, ok_out in (
+            (UP, has_up & (place <= z), (place > 0) | (z < line - 2)),
+            (DOWN, has_down & (place >= z), (place < line - 1) | (z > 1)),
+            (PARTNER, s != f, jnp.logical_not(skipped)),
         ):
-
-            @pl.when(ok)
-            def _():
-                for m in range(2):
-                    for j in range(2):
-                        way_copy(way, m, s, j).wait_send()
-
+            for m in range(2):
+
+                @pl.when(ok & ok_out if m == 1 else ok)
+                def _():
+                    for piece in range(2):
+                        way_copy(way, m, s, piece).wait_send()
+
+    @pl.loop(0, line)
+    def _(place):
+        @pl.when(jnp.logical_not(is_end & (place == far)))
+        def _():
+            for unit, (at, size) in enumerate(units):
+                for way in range(3):
+                    part_copy(way, place, at, size, unit).wait_send()
+
+    @pl.when(is_helper)
+    def _():
         for way in range(3):
-            part_copy(way, s).wait_send()
+            help_part(way).wait_send()
+        done_copy.wait_send()
+
+    @pl.when(is_end)
+    def _():
+        @pl.loop(0, groups)
+        def _(j):
+            attn_copy(j).wait_send()
 
     for way in range(3):
         len_copy(way).wait_send()
@@ -659,6 +811,7 @@
         and tokens.shape[1] == HEAD_SIZE
         and shards * groups <= HEAD_SIZE
         and out_weight.shape[1] % 64 == 0
+        and out_weight.shape[1] > HEAD_SIZE
     )
 
 
@@ -682,6 +835,7 @@
     key_cols = KEY_FEATURES // groups
     all_cols = query_cols + 2 * key_cols
     rows = groups * seq_rows
+    line, pair = shards // 2, 2 * out_cols
     cosine, sine = rotary_tables(seq_rows)
     everyone = shards * groups
     dma = pltpu.SemaphoreType.DMA
@@ -699,18 +853,24 @@
         out_specs=(vmem, scalar, scalar),
         scratch_shapes=[
             pltpu.VMEM((shards * depth, all_cols), bf16),
-            pltpu.VMEM((shards, out_cols, query_cols), bf16),
+            pltpu.VMEM((shards * out_cols, query_cols), bf16),
             pltpu.VMEM((2, depth // 4, all_cols), bf16),
-            pltpu.VMEM((2, out_cols // 4, query_cols), bf16),
+            pltpu.VMEM((2, out_pieces(out_cols)[0] // 2, query_cols), bf16),
             pltpu.VMEM((seq_rows, width), bf16),
             pltpu.VMEM((8, seq_rows), jnp.int32),
             pltpu.VMEM((groups, 8, seq_rows), jnp.int32),
             pltpu.VMEM((rows, width), bf16),
             pltpu.VMEM((rows, all_cols), f32),
             pltpu.VMEM((rows, query_cols), bf16),
-            pltpu.VMEM((shards, seq_rows, out_cols), f32),
-            pltpu.VMEM((shards, rows, out_cols), bf16),
-            pltpu.VMEM((groups - 1, shards, seq_rows, out_cols), bf16),
+            pltpu.VMEM((line, seq_rows, pair), f32),
+            pltpu.VMEM((line, rows, pair), bf16),
+            pltpu.VMEM((groups - 1, line, seq_rows, pair), bf16),
+            pltpu.VMEM((rows, query_cols), bf16),
+            pltpu.VMEM((seq_rows, pair), f32),
+            pltpu.VMEM((groups, seq_rows, pair), bf16),
+            pltpu.VMEM((groups - 1, seq_rows, pair), bf16),
+            pltpu.VMEM((seq_rows, pair), bf16),
+            pltpu.VMEM((seq_rows, pair), bf16),
             pltpu.VMEM((2, 8, HEAD_SIZE), f32),
             pltpu.VMEM((8, HEAD_SIZE), f32),
             pltpu.VMEM((everyone, 8, HEAD_SIZE), f32),
@@ -725,15 +885,20 @@
             pltpu.SMEM((1,), f32),
             pltpu.SMEM((everyone,), jnp.int32),
             dma((31,)),
-            dma((2, shards, 4)),
+            dma((2, shards, 2, 2)),
             dma((3, 2, shards, 2)),
             dma((2, 2)),
             dma((3, 2)),
             dma((3, 2)),
             dma((3,)),
             dma((3,)),
-            dma((3, shards)),
-            dma((3, shards)),
+            dma((3, line, 3)),
+            dma((3, line, 3)),
+            dma((groups,)),
+            dma((groups,)),
+            dma((3,)),
+            dma((3,)),
+            dma((2,)),
             dma((everyone,)),
             dma((everyone,)),
         ],

time: 147 us -> 135 us (0.918)
  Pallas kernels: 143 us -> 131 us
    pallas_call x1, Pallas kernels: 143 us -> 131 us  [layer(): pl.pallas_call(functools.partial(layer_kernel, shards, groups), out_shape...]
where the time goes in v3:
time: 135 us
  Pallas kernels  131 us (97%)
  between operations  2.97 us (2%)
    pallas_call x1, Pallas kernels, layer(): pl.pallas_call(functools.partial(layer_kernel, shards, groups), out_shape...  131 us

profile of v3, /device:TPU:0, one launch (start us, length us, event | category | flops | bytes accessed | tf_op | source)
XLA Modules:
  0.0 135.2 jit_solution(13138841283485948385)
XLA Ops:
  1.9 131.3 %shard_map.139 = (bf16[128,3584]{1,0:T(8,128)(2,1)S(1)}, f32[1]{0:T(128)S(4)}, f32[1]{0:T(128)S(4)}) custom-call(bf16[128,3584]{1,0:T(8,128)(2,1)} %bitcast.6, bf16[448,4608]{1,0:T(8,128)(2,1)} %qkv_weight.1, bf16[448,3584]{1,0:T(8,128)(2,1)} %bitcast.5, s32[1]{0:T(128)S(6)} %copy.21.length_one, f32[1]{0:T(128)S(6)} %copy.22.pair_weight_one, s32[32]{0:T(128)} %partner_all.1, ...), custom_call_target="tpu_custom_call" | custom-call | tf_op jit(solution)/shard_map/pallas_call | solution.py:845
  134.3 0.9 copy.18

commit v4 on v3

--- a/solution.py
+++ b/solution.py
@@ -116,8 +116,7 @@
     cosine_table,
     sine_table,
     hidden,
-    margin_out,
-    loss_out,
+    results,
     qkv_full,
     out_full,
     cross_qkv,
@@ -404,7 +403,7 @@
     tok_copy(0, 1).start()
     tok_copy(1, 0).start()
     length_load.wait()
-    len_tile[...] = jnp.full(len_tile.shape, length[0], jnp.int32)
+    len_tile[...] = jnp.full(len_tile.shape, length[0, 0], jnp.int32)
     len_all[0] = len_tile[...]
     for way in range(3):
         len_copy(way).start()
@@ -503,6 +502,34 @@
     key_heads = key_cols // HEAD_SIZE
     share = heads // key_heads
 
+    def lanes_of(at, size):
+        return pl.ds(pl.multiple_of(at, HEAD_SIZE), size)
+
+    units = ((0, big), (big, 2 * small), (pair - big, big))
+
+    def part_copy(way, place, at, size, unit):
+        cols = lanes_of(at, size)
+        return pltpu.make_async_remote_copy(
+            src_ref=part_out.at[place, pl.ds((1 + way) * seq_rows, seq_rows), cols],
+            dst_ref=part_in.at[way, place, :, cols],
+            send_sem=part_send.at[way, place, unit],
+            recv_sem=part_recv.at[way, place, unit],
+            device_id=team_ids[way],
+        )
+
+    def project(place, at, size, unit):
+        cols = lanes_of(at, size)
+        result = lax.dot_general(
+            attn[...],
+            out_full[lanes_of(place * pair + at, size), :],
+            (((1,), (1,)), ((), ())),
+            preferred_element_type=jnp.float32,
+        )
+        part_out[place, :, cols] = result.astype(jnp.bfloat16)
+        own[place, :, cols] = result[:seq_rows]
+        for way in (2, 0, 1):
+            part_copy(way, place, at, size, unit).start()
+
     def attn_copy(j):
         rows = pl.ds(pl.multiple_of(j * seq_rows, seq_rows), seq_rows)
         return pltpu.make_async_remote_copy(
@@ -512,6 +539,8 @@
             recv_sem=attn_recv.at[j],
             device_id=end_to_helper,
         )
+
+    from_partner(1, across)
 
     @pl.loop(0, groups)
     def _(i):
@@ -528,42 +557,25 @@
                 query = rotate(head_rows(j, h * HEAD_SIZE))
                 scores = lax.dot_general(
                     query, key, (((1,), (1,)), ((), ())), preferred_element_type=jnp.float32
-                ) / np.float32(np.sqrt(HEAD_SIZE))
+                ) * np.float32(1 / np.sqrt(HEAD_SIZE))
                 scores = jnp.where(allowed, scores, jnp.float32(-1e30))
                 expd = jnp.exp(scores - jnp.max(scores, axis=-1, keepdims=True))
-                probs = (expd / jnp.sum(expd, axis=-1, keepdims=True)).astype(jnp.bfloat16)
+                inverse = 1.0 / jnp.sum(expd, axis=-1, keepdims=True)
+                probs = (expd * inverse).astype(jnp.bfloat16)
                 attn[at, h * HEAD_SIZE : (h + 1) * HEAD_SIZE] = jnp.dot(
                     probs, value, preferred_element_type=jnp.float32
                 ).astype(jnp.bfloat16)
         pl.when(is_end)(attn_copy(j).start)
-
-    def lanes_of(at, size):
-        return pl.ds(pl.multiple_of(at, HEAD_SIZE), size)
-
-    units = ((0, big), (big, 2 * small), (pair - big, big))
-
-    def part_copy(way, place, at, size, unit):
-        cols = lanes_of(at, size)
-        return pltpu.make_async_remote_copy(
-            src_ref=part_out.at[place, pl.ds((1 + way) * seq_rows, seq_rows), cols],
-            dst_ref=part_in.at[way, place, :, cols],
-            send_sem=part_send.at[way, place, unit],
-            recv_sem=part_recv.at[way, place, unit],
-            device_id=team_ids[way],
-        )
-
-    def project(place, at, size, unit):
-        cols = lanes_of(at, size)
         result = lax.dot_general(
-            attn[...],
-            out_full[lanes_of(place * pair + at, size), :],
+            attn[at, :],
+            out_full[lanes_of(z * pair, pair), :],
             (((1,), (1,)), ((), ())),
             preferred_element_type=jnp.float32,
         )
-        part_out[place, :, cols] = result.astype(jnp.bfloat16)
-        own[place, :, cols] = result[:seq_rows]
-        for way in (2, 0, 1):
-            part_copy(way, place, at, size, unit).start()
+        part_out[z, at, :] = result.astype(jnp.bfloat16)
+        own[z] = result
+        for way in range(3):
+            pl.when(j == way + 1)(part_copy(way, z, 0, pair, 0).start)
 
     def project_pair(place):
         @pl.loop(0, 2)
@@ -587,10 +599,20 @@
             stats[0] += squares[:, lanes]
             stats[1] += weighted[:, lanes]
 
+    def each_part(place, body):
+        @pl.when(place == z)
+        def _():
+            for way in range(3):
+                body(part_copy(way, place, 0, pair, 0))
+
+        @pl.when(place != z)
+        def _():
+            for unit, (at, size) in enumerate(units):
+                for way in range(3):
+                    body(part_copy(way, place, at, size, unit))
+
     def finish_parts(place):
-        for unit, (at, size) in enumerate(units):
-            for way in range(3):
-                part_copy(way, place, at, size, unit).wait_recv()
+        each_part(place, lambda copy: copy.wait_recv())
         total = own[place]
         for way in range(3):
             total += part_in[way, place].astype(jnp.float32)
@@ -617,9 +639,6 @@
     def cross_unit(place):
         arrived(1, 2 * place + 1 - y, 0, 1 - core)
         project(place, (1 - y) * (pair - big), big, 2 * (1 - y))
-
-    from_partner(1, across)
-    project_pair(z)
 
     @pl.loop(1, line - 1)
     def _(k):
@@ -712,7 +731,7 @@
     mean = jnp.sum(stats[0], axis=-1, keepdims=True) / width
     score = jnp.sum(stats[1], axis=-1, keepdims=True) * lax.rsqrt(mean + 1e-06)
     first_row = lax.broadcasted_iota(jnp.int32, score_tile.shape, 0) == 0
-    score_tile[...] = jnp.where(first_row, score, jnp.full(score_tile.shape, pair_weight[0]))
+    score_tile[...] = jnp.where(first_row, score, jnp.full(score_tile.shape, pair_weight[0, 0]))
     score_all[me] = score_tile[...]
 
     def score_copy(i):
@@ -753,9 +772,7 @@
     def _(place):
         @pl.when(jnp.logical_not(is_end & (place == far)))
         def _():
-            for unit, (at, size) in enumerate(units):
-                for way in range(3):
-                    part_copy(way, place, at, size, unit).wait_send()
+            each_part(place, lambda copy: copy.wait_send())
 
     @pl.when(is_helper)
     def _():
@@ -793,8 +810,7 @@
     first_lane = lane == 0
     margin = jnp.sum(jnp.where(first_lane & (row == me), margins, 0.0))
     loss = jnp.sum(jnp.where(first_lane, weights * softplus, 0.0)) / everyone
-    margin_out[0] = margin
-    loss_out[0] = loss
+    results[...] = jnp.where(first_row, jnp.full(results.shape, margin), loss)
 
     @pl.loop(1, everyone)
     def _(i):
@@ -840,17 +856,15 @@
     everyone = shards * groups
     dma = pltpu.SemaphoreType.DMA
     vmem = pl.BlockSpec(memory_space=pltpu.VMEM)
-    scalar = pl.BlockSpec(memory_space=pltpu.SMEM)
     bf16, f32 = jnp.bfloat16, jnp.float32
-    hidden, margin, loss = pl.pallas_call(
+    hidden, results = pl.pallas_call(
         functools.partial(layer_kernel, shards, groups),
         out_shape=(
             pltpu.VMEM((seq_rows, width), bf16),
-            pltpu.SMEM((1,), f32),
-            pltpu.SMEM((1,), f32),
+            pltpu.VMEM((8, HEAD_SIZE), f32),
         ),
         in_specs=[pl.BlockSpec(memory_space=pltpu.HBM)] * 12,
-        out_specs=(vmem, scalar, scalar),
+        out_specs=(vmem, vmem),
         scratch_shapes=[
             pltpu.VMEM((shards * depth, all_cols), bf16),
             pltpu.VMEM((shards * out_cols, query_cols), bf16),
@@ -881,8 +895,8 @@
             pltpu.VMEM((1, qkv_bias.shape[0] + 8 * HEAD_SIZE), f32),
             pltpu.VMEM((seq_rows, HEAD_SIZE), f32),
             pltpu.VMEM((seq_rows, HEAD_SIZE), f32),
-            pltpu.SMEM((1,), jnp.int32),
-            pltpu.SMEM((1,), f32),
+            pltpu.SMEM((1, 1), jnp.int32),
+            pltpu.SMEM((1, 1), f32),
             pltpu.SMEM((everyone,), jnp.int32),
             dma((31,)),
             dma((2, shards, 2, 2)),
@@ -909,8 +923,8 @@
         tokens[0],
         qkv_weight,
         out_weight.T,
-        lengths,
-        pair_weight,
+        lengths[None],
+        pair_weight[None],
         partner,
         norm_gain,
         final_gain,
@@ -919,7 +933,7 @@
         jnp.asarray(cosine),
         jnp.asarray(sine),
     )
-    return hidden[None], margin, loss.reshape(())
+    return hidden[None], results[0, :1], results[1, 0]
 
 
 def projected_by_gathers(

time: 135 us -> 128 us (0.948)
  Pallas kernels: 131 us -> 124 us
    pallas_call x1, Pallas kernels: 131 us -> 124 us  [layer(): pl.pallas_call(functools.partial(layer_kernel, shards, groups), out_shape...]
where the time goes in v4:
time: 128 us
  Pallas kernels  124 us (97%)
  between operations  1.93 us (2%)
  local copies, waits for them, and re-layouts  1.44 us (1%)
    pallas_call x1, Pallas kernels, layer(): pl.pallas_call(functools.partial(layer_kernel, shards, groups), out_shape...  124 us

profile of v4, /device:TPU:0, one launch (start us, length us, event | category | flops | bytes accessed | tf_op | source)
XLA Modules:
  0.0 127.6 jit_solution(3316883225137332863)
XLA Ops:
  1.9 124.2 %shard_map.139 = (bf16[128,3584]{1,0:T(8,128)(2,1)S(1)}, f32[8,128]{1,0:T(8,128)S(1)}) custom-call(bf16[128,3584]{1,0:T(8,128)(2,1)} %bitcast.11, bf16[448,4608]{1,0:T(8,128)(2,1)} %qkv_weight.1, bf16[448,3584]{1,0:T(8,128)(2,1)} %bitcast.10, s32[1,1]{1,0:T(1,128)} %bitcast.7.length_one, f32[1,1]{1,0:T(1,128)} %bitcast.8.pair_weight_one, s32[32]{0:T(128)} %partner_all.1, ...), custom_call_target="tpu_custom_call" | custom-call | tf_op jit(solution)/shard_map/pallas_call | solution.py:860
  126.2 0.5 fusion
  126.7 0.9 copy.16

commit v5 on v4

--- a/solution.py
+++ b/solution.py
@@ -137,6 +137,8 @@
     help_sum,
     help_done,
     stats,
+    queries,
+    score_rows,
     score_tile,
     score_all,
     partner_rows,
@@ -155,8 +157,7 @@
     cross_send,
     tok_send,
     tok_recv,
-    len_send,
-    len_recv,
+    len_sem,
     part_send,
     part_recv,
     attn_send,
@@ -164,8 +165,7 @@
     help_send,
     help_recv,
     done_sem,
-    score_send,
-    score_recv,
+    score_sem,
 ):
     line = shards // 2
     f = lax.axis_index("fsdp")
@@ -228,19 +228,24 @@
         copy.start()
         return copy
 
+    def bytes_of(ref, sem):
+        return pltpu.make_async_copy(ref, ref, sem)
+
     def qkv_parts(piece, half, owner, dest):
+        nonlocal count
         rows = pl.ds(pl.multiple_of((2 * piece + half) * quarter, 16), quarter)
-        return [
-            local(
+        for start, size, to in (
+            (owner * query_cols, query_cols, 0),
+            (QUERY_FEATURES + owner * key_cols, key_cols, query_cols),
+            (QUERY_FEATURES + KEY_FEATURES + owner * key_cols, key_cols, query_cols + key_cols),
+        ):
+            pltpu.make_async_copy(
                 qkv_weight.at[rows, pl.ds(pl.multiple_of(start, 128), size)],
                 dest.at[:, pl.ds(to, size)],
-            )
-            for start, size, to in (
-                (owner * query_cols, query_cols, 0),
-                (QUERY_FEATURES + owner * key_cols, key_cols, query_cols),
-                (QUERY_FEATURES + KEY_FEATURES + owner * key_cols, key_cols, query_cols + key_cols),
-            )
-        ]
+                local_sem.at[count],
+            ).start()
+        count += 1
+        return bytes_of(dest, local_sem.at[count - 1])
 
     length_load = local(length_one, length)
     own_loads, cross_loads = [], []
@@ -259,7 +264,7 @@
     ]
     late_loads = []
     for j in range(2):
-        late_loads.extend(qkv_parts(j, 1 - core, team, slot(0, f, j, 1 - core)))
+        late_loads.append(qkv_parts(j, 1 - core, team, slot(0, f, j, 1 - core)))
     out_own = local(
         out_weight.at[:, pl.ds(pl.multiple_of(team * query_cols, 128), query_cols)],
         out_full.at[pl.ds(pl.multiple_of(f * out_cols, 16), out_cols)],
@@ -300,7 +305,7 @@
         return pltpu.make_async_remote_copy(
             src_ref=slot(m, s, piece, core),
             dst_ref=slot(m, s, piece, core),
-            send_sem=send_sem.at[way, m, s, piece],
+            send_sem=send_sem.at[way, m],
             recv_sem=recv_sem.at[m, s, piece, core],
             device_id=way_ids[way],
         )
@@ -313,7 +318,7 @@
         return pltpu.make_async_remote_copy(
             src_ref=cross_part(m, j),
             dst_ref=slot(m, f, piece, core),
-            send_sem=cross_send.at[m, j],
+            send_sem=cross_send.at[m],
             recv_sem=recv_sem.at[m, f, piece, core],
             device_id=team_ids[1],
         )
@@ -356,16 +361,17 @@
         for piece in range(2):
             arrived(m, s, piece, 1 - core)
 
-    half_rows = seq_rows // 2
-
-    def tok_copy(way, half):
-        source = (0, 0, 1 + half)[way]
-        target = team_ids[way] if way < 2 else team_ids[1 - half]
+    tok_starts = (0, seq_rows // 4, seq_rows * 5 // 8, seq_rows)
+
+    def tok_copy(way, piece):
+        source = 0 if way < 2 else (1, 2, 2)[piece]
+        target = team_ids[way] if way < 2 else team_ids[(1, 0, 0)[piece]]
+        start, size = tok_starts[piece], tok_starts[piece + 1] - tok_starts[piece]
         return pltpu.make_async_remote_copy(
-            src_ref=normed.at[pl.ds(source * seq_rows + half * half_rows, half_rows)],
-            dst_ref=normed.at[pl.ds((1 + way) * seq_rows + half * half_rows, half_rows)],
-            send_sem=tok_send.at[way, half],
-            recv_sem=tok_recv.at[way, half],
+            src_ref=normed.at[pl.ds(source * seq_rows + start, size)],
+            dst_ref=normed.at[pl.ds((1 + way) * seq_rows + start, size)],
+            send_sem=tok_send.at[way],
+            recv_sem=tok_recv.at[way, piece],
             device_id=target,
         )
 
@@ -373,17 +379,15 @@
         return pltpu.make_async_remote_copy(
             src_ref=len_tile,
             dst_ref=len_all.at[1 + way],
-            send_sem=len_send.at[way],
-            recv_sem=len_recv.at[way],
+            send_sem=len_sem.at[0],
+            recv_sem=len_sem.at[1],
             device_id=team_ids[way],
         )
 
     for j in range(2):
-        for copy in own_loads[j]:
-            copy.wait()
+        own_loads[j].wait()
         send_both(0, f, j)
-        for copy in cross_loads[j]:
-            copy.wait()
+        cross_loads[j].wait()
         cross_copy(0, j).start()
 
     tok_local.wait()
@@ -398,10 +402,9 @@
         scale = lax.rsqrt(jnp.mean(rows * rows, axis=-1, keepdims=True) + 1e-06)
         normed[at, :] = (rows * scale * norm_gain[...]).astype(jnp.bfloat16)
 
-    tok_copy(0, 0).start()
-    tok_copy(1, 1).start()
-    tok_copy(0, 1).start()
-    tok_copy(1, 0).start()
+    for first, second in ((0, 1), (1, 2), (2, 0)):
+        tok_copy(0, first).start()
+        tok_copy(1, second).start()
     length_load.wait()
     len_tile[...] = jnp.full(len_tile.shape, length[0, 0], jnp.int32)
     len_all[0] = len_tile[...]
@@ -424,27 +427,21 @@
         line_step(0, 1, 0, j)
     tok_copy(0, 0).wait_recv()
     tok_copy(2, 0).start()
-    line_step(0, 1, 1, 0)
-    line_step(0, 1, 1, 1)
-    tok_copy(1, 1).wait_recv()
-    tok_copy(2, 1).start()
     out_own.wait()
     for j in range(2):
         out_cross[j].wait()
         cross_copy(1, j).start()
-    for k in range(2, line - 1):
-        for o in range(2):
-            for j in range(2):
-                line_step(0, k, o, j)
     for j in range(2):
-        send_both(1, f, j)
-
-    tok_copy(0, 1).wait_recv()
-    tok_copy(1, 0).wait_recv()
-    tok_copy(2, 0).wait_recv()
-    tok_copy(2, 1).wait_recv()
-    for way in range(3):
-        len_copy(way).wait_recv()
+        line_step(0, 1, 1, j)
+        tok_copy(1, 1 + j).wait_recv()
+        tok_copy(2, 1 + j).start()
+    steps = [(k, o, j) for k in range(2, line - 1) for o in range(2) for j in range(2)]
+    for k, o, j in steps[:-1]:
+        line_step(0, k, o, j)
+
+    for way, piece in ((0, 1), (0, 2), (1, 0), (2, 0), (2, 1), (2, 2)):
+        tok_copy(way, piece).wait_recv()
+    bytes_of(len_all.at[pl.ds(1, 3)], len_sem.at[1]).wait()
     for copy in (*late_loads, *small_loads):
         copy.wait()
 
@@ -452,17 +449,12 @@
     def _(i):
         partner_rows[pl.ds(i, 1), :] = jnp.full((1, HEAD_SIZE), partner[i], jnp.int32)
 
-    tile = 3 * HEAD_SIZE
-
     def qkv_step(place):
         rows = pl.ds(pl.multiple_of(place * 2 * depth, 128), 2 * depth)
 
-        @pl.loop(0, (query_cols + 2 * key_cols) // tile)
-        def _(t):
-            cols = pl.ds(pl.multiple_of(t * tile, tile), tile)
-            qkv_rows[:, cols] += jnp.dot(
-                normed[:, rows], qkv_full[rows, cols], preferred_element_type=jnp.float32
-            )
+        qkv_rows[...] += jnp.dot(
+            normed[:, rows], qkv_full[rows, :], preferred_element_type=jnp.float32
+        )
 
     def qkv_places(first, last):
         @pl.loop(2 * first, 2 * last)
@@ -481,7 +473,11 @@
         from_partner(0, across)
         qkv_step(z)
 
-    qkv_places(1, line - 1)
+    qkv_places(1, 2)
+    line_step(0, *steps[-1])
+    for j in range(2):
+        send_both(1, f, j)
+    qkv_places(2, line - 1)
     for j in range(2):
         cross_step(1, j)
     for o in range(2):
@@ -512,8 +508,8 @@
         return pltpu.make_async_remote_copy(
             src_ref=part_out.at[place, pl.ds((1 + way) * seq_rows, seq_rows), cols],
             dst_ref=part_in.at[way, place, :, cols],
-            send_sem=part_send.at[way, place, unit],
-            recv_sem=part_recv.at[way, place, unit],
+            send_sem=part_send.at[way],
+            recv_sem=part_recv.at[way, place],
             device_id=team_ids[way],
         )
 
@@ -535,12 +531,10 @@
         return pltpu.make_async_remote_copy(
             src_ref=attn.at[rows],
             dst_ref=attn_help.at[rows],
-            send_sem=attn_send.at[j],
+            send_sem=attn_send.at[0],
             recv_sem=attn_recv.at[j],
             device_id=end_to_helper,
         )
-
-    from_partner(1, across)
 
     @pl.loop(0, groups)
     def _(i):
@@ -551,21 +545,32 @@
         at = pl.ds(pl.multiple_of(j * seq_rows, seq_rows), seq_rows)
         for kh in range(key_heads):
             offset = kh * HEAD_SIZE
+            group = [slice(h * HEAD_SIZE, (h + 1) * HEAD_SIZE) for h in range(share)]
+            first = kh * share * HEAD_SIZE
             key = rotate(head_rows(j, query_cols + offset))
             value = head_rows(j, query_cols + key_cols + offset).astype(jnp.bfloat16)
-            for h in range(kh * share, (kh + 1) * share):
-                query = rotate(head_rows(j, h * HEAD_SIZE))
-                scores = lax.dot_general(
-                    query, key, (((1,), (1,)), ((), ())), preferred_element_type=jnp.float32
-                ) * np.float32(1 / np.sqrt(HEAD_SIZE))
+            for lanes in group:
+                queries[lanes, :] = rotate(head_rows(j, first + lanes.start))
+            score_rows[...] = lax.dot_general(
+                queries[...], key, (((1,), (1,)), ((), ())), preferred_element_type=jnp.float32
+            )
+            for lanes in group:
+                scores = score_rows[lanes, :] * np.float32(1 / np.sqrt(HEAD_SIZE))
                 scores = jnp.where(allowed, scores, jnp.float32(-1e30))
                 expd = jnp.exp(scores - jnp.max(scores, axis=-1, keepdims=True))
                 inverse = 1.0 / jnp.sum(expd, axis=-1, keepdims=True)
-                probs = (expd * inverse).astype(jnp.bfloat16)
-                attn[at, h * HEAD_SIZE : (h + 1) * HEAD_SIZE] = jnp.dot(
-                    probs, value, preferred_element_type=jnp.float32
-                ).astype(jnp.bfloat16)
+                queries[lanes, :] = (expd * inverse).astype(jnp.bfloat16)
+            mixed = jnp.dot(queries[...], value, preferred_element_type=jnp.float32)
+            for lanes in group:
+                attn[at, first + lanes.start : first + lanes.stop] = mixed[lanes].astype(
+                    jnp.bfloat16
+                )
         pl.when(is_end)(attn_copy(j).start)
+
+        @pl.when(i == 0)
+        def _():
+            from_partner(1, across)
+
         result = lax.dot_general(
             attn[at, :],
             out_full[lanes_of(z * pair, pair), :],
@@ -599,20 +604,9 @@
             stats[0] += squares[:, lanes]
             stats[1] += weighted[:, lanes]
 
-    def each_part(place, body):
-        @pl.when(place == z)
-        def _():
-            for way in range(3):
-                body(part_copy(way, place, 0, pair, 0))
-
-        @pl.when(place != z)
-        def _():
-            for unit, (at, size) in enumerate(units):
-                for way in range(3):
-                    body(part_copy(way, place, at, size, unit))
-
     def finish_parts(place):
-        each_part(place, lambda copy: copy.wait_recv())
+        for way in range(3):
+            bytes_of(part_in.at[way, place], part_recv.at[way, place]).wait()
         total = own[place]
         for way in range(3):
             total += part_in[way, place].astype(jnp.float32)
@@ -670,7 +664,7 @@
         return pltpu.make_async_remote_copy(
             src_ref=help_out.at[1 + way],
             dst_ref=help_in.at[way],
-            send_sem=help_send.at[way],
+            send_sem=help_send.at[0],
             recv_sem=help_recv.at[way],
             device_id=team_ids[way],
         )
@@ -739,8 +733,8 @@
         return pltpu.make_async_remote_copy(
             src_ref=score_tile,
             dst_ref=score_all.at[me],
-            send_sem=score_send.at[other],
-            recv_sem=score_recv.at[me],
+            send_sem=score_sem.at[0],
+            recv_sem=score_sem.at[1],
             device_id={"fsdp": other // groups, "dp": lax.rem(other, groups)},
         )
 
@@ -748,55 +742,40 @@
     def _(i):
         score_copy(i).start()
 
-    for m in range(2):
-        for j in range(2):
-            cross_copy(m, j).wait_send()
-
-    @pl.loop(0, shards)
-    def _(s):
-        place = s // 2
-        skipped = (place == far) & is_end
-        for way, ok, ok_out in (
-            (UP, has_up & (place <= z), (place > 0) | (z < line - 2)),
-            (DOWN, has_down & (place >= z), (place < line - 1) | (z > 1)),
-            (PARTNER, s != f, jnp.logical_not(skipped)),
-        ):
-            for m in range(2):
-
-                @pl.when(ok & ok_out if m == 1 else ok)
-                def _():
-                    for piece in range(2):
-                        way_copy(way, m, s, piece).wait_send()
-
-    @pl.loop(0, line)
-    def _(place):
-        @pl.when(jnp.logical_not(is_end & (place == far)))
+    bytes_of(cross_qkv, cross_send.at[0]).wait()
+    bytes_of(out_full.at[pl.ds(0, out_cols // 2)], cross_send.at[1]).wait()
+    bytes_of(len_all.at[pl.ds(1, 3)], len_sem.at[0]).wait()
+    for way in range(3):
+        bytes_of(normed.at[pl.ds(0, seq_rows)], tok_send.at[way]).wait()
+    for spot in range(line):
+        ends = spot in (0, line - 1)
+        up = 0 if spot == line - 1 else 2 * (spot + 1)
+        down = 0 if spot == 0 else 2 * (line - spot)
+        sent = (
+            (UP, up, up - 2 * (spot == line - 2)),
+            (DOWN, down, down - 2 * (spot == 1)),
+            (PARTNER, shards - 1, shards - 1 - 2 * ends),
+        )
+
+        @pl.when(z == spot)
         def _():
-            each_part(place, lambda copy: copy.wait_send())
+            for way, slices, out_slices in sent:
+                if slices:
+                    rows = pl.ds(0, slices * depth // 2)
+                    bytes_of(qkv_full.at[rows], send_sem.at[way, 0]).wait()
+                    rows = pl.ds(0, out_slices * out_cols // 2)
+                    bytes_of(out_full.at[rows], send_sem.at[way, 1]).wait()
+            for way in range(3):
+                bytes_of(part_in.at[0, pl.ds(0, line - ends)], part_send.at[way]).wait()
+            if ends:
+                bytes_of(attn, attn_send.at[0]).wait()
 
     @pl.when(is_helper)
     def _():
-        for way in range(3):
-            help_part(way).wait_send()
+        bytes_of(help_in, help_send.at[0]).wait()
         done_copy.wait_send()
 
-    @pl.when(is_end)
-    def _():
-        @pl.loop(0, groups)
-        def _(j):
-            attn_copy(j).wait_send()
-
-    for way in range(3):
-        len_copy(way).wait_send()
-        for half in range(2):
-            tok_copy(way, half).wait_send()
-
-    @pl.loop(1, everyone)
-    def _(i):
-        other = lax.rem(me + i, everyone)
-        pltpu.make_async_copy(
-            score_all.at[other], score_all.at[other], score_recv.at[other]
-        ).wait()
+    bytes_of(score_all.at[pl.ds(0, everyone - 1)], score_sem.at[1]).wait()
 
     scores = score_all[:, 0, :]
     weights = score_all[:, 1, :]
@@ -811,10 +790,7 @@
     margin = jnp.sum(jnp.where(first_lane & (row == me), margins, 0.0))
     loss = jnp.sum(jnp.where(first_lane, weights * softplus, 0.0)) / everyone
     results[...] = jnp.where(first_row, jnp.full(results.shape, margin), loss)
-
-    @pl.loop(1, everyone)
-    def _(i):
-        score_copy(i).wait_send()
+    bytes_of(score_all.at[pl.ds(0, everyone - 1)], score_sem.at[0]).wait()
 
 
 def layer_fits(shards, groups, tokens, qkv_weight, out_weight):
@@ -886,6 +862,8 @@
             pltpu.VMEM((seq_rows, pair), bf16),
             pltpu.VMEM((seq_rows, pair), bf16),
             pltpu.VMEM((2, 8, HEAD_SIZE), f32),
+            pltpu.VMEM((query_cols * HEAD_SIZE // key_cols, HEAD_SIZE), bf16),
+            pltpu.VMEM((query_cols * HEAD_SIZE // key_cols, HEAD_SIZE), f32),
             pltpu.VMEM((8, HEAD_SIZE), f32),
             pltpu.VMEM((everyone, 8, HEAD_SIZE), f32),
             pltpu.VMEM((everyone, HEAD_SIZE), jnp.int32),
@@ -898,23 +876,21 @@
             pltpu.SMEM((1, 1), jnp.int32),
             pltpu.SMEM((1, 1), f32),
             pltpu.SMEM((everyone,), jnp.int32),
-            dma((31,)),
+            dma((19,)),
             dma((2, shards, 2, 2)),
-            dma((3, 2, shards, 2)),
-            dma((2, 2)),
             dma((3, 2)),
-            dma((3, 2)),
+            dma((2,)),
             dma((3,)),
+            dma((3, 3)),
+            dma((2,)),
             dma((3,)),
-            dma((3, line, 3)),
-            dma((3, line, 3)),
+            dma((3, line)),
+            dma((1,)),
             dma((groups,)),
-            dma((groups,)),
-            dma((3,)),
+            dma((1,)),
             dma((3,)),
             dma((2,)),
-            dma((everyone,)),
-            dma((everyone,)),
+            dma((2,)),
         ],
         compiler_params=pltpu.CompilerParams(
             collective_id=0, has_side_effects=True, vmem_limit_bytes=56 * 1024 * 1024

time: 128 us -> 124 us (0.969)
  Pallas kernels: 124 us -> 121 us
    pallas_call x1, Pallas kernels: 124 us -> 121 us  [layer(): pl.pallas_call(functools.partial(layer_kernel, shards, groups), out_shape...]
where the time goes in v5:
time: 124 us
  Pallas kernels  121 us (98%)
  between operations  1.93 us (2%)
  local copies, waits for them, and re-layouts  1.44 us (1%)
    pallas_call x1, Pallas kernels, layer(): pl.pallas_call(functools.partial(layer_kernel, shards, groups), out_shape...  121 us

profile of v5, /device:TPU:0, one launch (start us, length us, event | category | flops | bytes accessed | tf_op | source)
XLA Modules:
  0.0 124.0 jit_solution(18067568157439548055)
XLA Ops:
  1.9 120.7 %shard_map.139 = (bf16[128,3584]{1,0:T(8,128)(2,1)S(1)}, f32[8,128]{1,0:T(8,128)S(1)}) custom-call(bf16[128,3584]{1,0:T(8,128)(2,1)} %bitcast.11, bf16[448,4608]{1,0:T(8,128)(2,1)} %qkv_weight.1, bf16[448,3584]{1,0:T(8,128)(2,1)} %bitcast.10, s32[1,1]{1,0:T(1,128)} %bitcast.7.length_one, f32[1,1]{1,0:T(1,128)} %bitcast.8.pair_weight_one, s32[32]{0:T(128)} %partner_all.1, ...), custom_call_target="tpu_custom_call" | custom-call | tf_op jit(solution)/shard_map/pallas_call | solution.py:836
  122.6 0.5 fusion
  123.1 0.9 copy.16

commit v6 on v5

--- a/solution.py
+++ b/solution.py
@@ -152,7 +152,8 @@
     pair_weight,
     partner,
     local_sem,
-    recv_sem,
+    qkv_recv,
+    out_recv,
     send_sem,
     cross_send,
     tok_send,
@@ -207,9 +208,17 @@
         def _():
             pl.semaphore_signal(barrier, inc=1, device_id=way_ids[way])
 
+    piece_sizes = (big, small, big // 2, big // 2)
+    pieces = (((0, 1), (0, 1)), ((0, 1), (1, 2, 3)))
+
     def out_rows(side, piece, half):
-        size = (big, small)[piece] // 2
-        start = (side * small, (1 - side) * big)[piece]
+        size = piece_sizes[piece] // 2
+        start = (
+            side * small,
+            (1 - side) * big,
+            (1 - side) * (big // 2) + side * small,
+            side * (small + big // 2),
+        )[piece]
         return start + half * size, size
 
     def slot(m, s, piece, half):
@@ -218,6 +227,11 @@
             return qkv_full.at[pl.ds(pl.multiple_of(start, 16), quarter)]
         start, size = out_rows(lax.rem(s, 2), piece, half)
         return out_full.at[pl.ds(pl.multiple_of(s * out_cols + start, 16), size)]
+
+    def recv_of(m, s, piece, by_partner):
+        if m == 0:
+            return qkv_recv.at[s, 2 if by_partner else piece]
+        return out_recv.at[s, (0, 1, 0, 2)[piece], by_partner]
 
     count = 0
 
@@ -273,11 +287,11 @@
     def cross_part(m, j):
         if m == 0:
             return cross_qkv.at[j]
-        return cross_out.at[j, pl.ds(0, (small, big)[j] // 2)]
+        return cross_out.at[j, pl.ds(0, piece_sizes[pieces[1][1][j]] // 2)]
 
     out_cross = []
-    for j in range(2):
-        start, size = out_rows(y, 1 - j, core)
+    for j, piece in enumerate(pieces[1][1]):
+        start, size = out_rows(y, piece, core)
         out_cross.append(
             local(
                 out_weight.at[
@@ -306,34 +320,30 @@
             src_ref=slot(m, s, piece, core),
             dst_ref=slot(m, s, piece, core),
             send_sem=send_sem.at[way, m],
-            recv_sem=recv_sem.at[m, s, piece, core],
+            recv_sem=recv_of(m, s, piece, int(way == PARTNER)),
             device_id=way_ids[way],
         )
 
-    def piece_of(m, o, j):
-        return 1 - j if m == 1 and o == 1 else j
-
     def cross_copy(m, j):
-        piece = piece_of(m, 1, j)
+        piece = pieces[m][1][j]
         return pltpu.make_async_remote_copy(
             src_ref=cross_part(m, j),
             dst_ref=slot(m, f, piece, core),
             send_sem=cross_send.at[m],
-            recv_sem=recv_sem.at[m, f, piece, core],
+            recv_sem=recv_of(m, f, piece, 0),
             device_id=team_ids[1],
         )
 
-    def arrived(m, s, piece, half):
-        there = slot(m, s, piece, half)
-        pltpu.make_async_copy(there, there, recv_sem.at[m, s, piece, half]).wait()
+    def arrived(m, s, piece, by_partner=0):
+        bytes_of(slot(m, s, piece, core), recv_of(m, s, piece, by_partner)).wait()
 
     def send_both(m, s, piece):
         pl.when(has_up)(way_copy(UP, m, s, piece).start)
         pl.when(has_down)(way_copy(DOWN, m, s, piece).start)
 
     def cross_step(m, j):
-        piece = piece_of(m, 1, j)
-        arrived(m, across, piece, core)
+        piece = pieces[m][1][j]
+        arrived(m, across, piece)
         send_both(m, across, piece)
         way_copy(PARTNER, m, across, piece).start()
 
@@ -346,20 +356,23 @@
         )
 
     def line_step(m, k, o, j):
-        piece = piece_of(m, o, j)
+        piece = pieces[m][o][j]
         for ok, s, way, onward in sides(k, o):
             if m == 1:
                 onward = onward & (k < line - 2)
 
             @pl.when(ok)
             def _():
-                arrived(m, s, piece, core)
+                arrived(m, s, piece)
                 pl.when(onward)(way_copy(way, m, s, piece).start)
                 way_copy(PARTNER, m, s, piece).start()
 
-    def from_partner(m, s):
-        for piece in range(2):
-            arrived(m, s, piece, 1 - core)
+    def from_partner(m, s, o=0):
+        if m == 0:
+            bytes_of(qkv_full.at[pl.ds(0, 2 * quarter)], qkv_recv.at[s, 2]).wait()
+        else:
+            for piece in pieces[1][o]:
+                arrived(1, s, piece, 1)
 
     tok_starts = (0, seq_rows // 4, seq_rows * 5 // 8, seq_rows)
 
@@ -428,7 +441,7 @@
     tok_copy(0, 0).wait_recv()
     tok_copy(2, 0).start()
     out_own.wait()
-    for j in range(2):
+    for j in range(3):
         out_cross[j].wait()
         cross_copy(1, j).start()
     for j in range(2):
@@ -478,7 +491,7 @@
     for j in range(2):
         send_both(1, f, j)
     qkv_places(2, line - 1)
-    for j in range(2):
+    for j in range(3):
         cross_step(1, j)
     for o in range(2):
         for j in range(2):
@@ -569,7 +582,7 @@
 
         @pl.when(i == 0)
         def _():
-            from_partner(1, across)
+            from_partner(1, across, 1)
 
         result = lax.dot_general(
             attn[at, :],
@@ -622,17 +635,23 @@
                 body(place)
 
     def own_unit(place):
-        arrived(1, 2 * place + y, 0, 1 - core)
+        arrived(1, 2 * place + y, 0, 1)
         project(place, y * (pair - big), big, 2 * y)
 
     def mid_unit(place):
-        arrived(1, 2 * place + y, 1, 1 - core)
-        arrived(1, 2 * place + 1 - y, 1, 1 - core)
+        arrived(1, 2 * place + y, 1, 1)
+        arrived(1, 2 * place + 1 - y, 1, 1)
         project(place, big, 2 * small, 1)
 
-    def cross_unit(place):
-        arrived(1, 2 * place + 1 - y, 0, 1 - core)
-        project(place, (1 - y) * (pair - big), big, 2 * (1 - y))
+    def cross_unit(piece):
+        inner = (1 - y) * (pair - big) + y * (big // 2)
+        outer = (1 - y) * (pair - big // 2)
+
+        def body(place):
+            arrived(1, 2 * place + 1 - y, piece, 1)
+            project(place, (inner, outer)[piece - 2], big // 2, 0)
+
+        return body
 
     @pl.loop(1, line - 1)
     def _(k):
@@ -654,11 +673,12 @@
         def _():
             at_sides(k, mid_unit)
 
-        line_step(1, k, 1, 1)
-
-        @pl.when(mine)
-        def _():
-            at_sides(k, cross_unit)
+        for j in (1, 2):
+            line_step(1, k, 1, j)
+
+            @pl.when(mine)
+            def _():
+                at_sides(k, cross_unit(1 + j))
 
     def help_part(way):
         return pltpu.make_async_remote_copy(
@@ -679,8 +699,8 @@
 
     @pl.when(is_helper)
     def _():
-        for o in range(2):
-            from_partner(1, 2 * far + o)
+        from_partner(1, 2 * far + y, 0)
+        from_partner(1, 2 * far + 1 - y, 1)
 
         @pl.loop(0, groups)
         def _(i):
@@ -845,7 +865,7 @@
             pltpu.VMEM((shards * depth, all_cols), bf16),
             pltpu.VMEM((shards * out_cols, query_cols), bf16),
             pltpu.VMEM((2, depth // 4, all_cols), bf16),
-            pltpu.VMEM((2, out_pieces(out_cols)[0] // 2, query_cols), bf16),
+            pltpu.VMEM((3, max(out_pieces(out_cols)) // 2, query_cols), bf16),
             pltpu.VMEM((seq_rows, width), bf16),
             pltpu.VMEM((8, seq_rows), jnp.int32),
             pltpu.VMEM((groups, 8, seq_rows), jnp.int32),
@@ -876,8 +896,9 @@
             pltpu.SMEM((1, 1), jnp.int32),
             pltpu.SMEM((1, 1), f32),
             pltpu.SMEM((everyone,), jnp.int32),
-            dma((19,)),
-            dma((2, shards, 2, 2)),
+            dma((20,)),
+            dma((shards, 3)),
+            dma((shards, 3, 2)),
             dma((3, 2)),
             dma((2,)),
             dma((3,)),

time: 124 us -> 124 us (level)
  no operation moved by 1% of the time
where the time goes in v6:
time: 124 us; the launch traced here: 123 us
  Pallas kernels  120 us (97%)
  between operations  1.93 us (2%)
  local copies, waits for them, and re-layouts  1.44 us (1%)
    pallas_call x1, Pallas kernels, layer(): pl.pallas_call(functools.partial(layer_kernel, shards, groups), out_shape...  120 us

profile of v6, /device:TPU:0, one launch (start us, length us, event | category | flops | bytes accessed | tf_op | source)
XLA Modules:
  0.0 123.4 jit_solution(16813852753457187297)
XLA Ops:
  1.9 120.0 %shard_map.139 = (bf16[128,3584]{1,0:T(8,128)(2,1)S(1)}, f32[8,128]{1,0:T(8,128)S(1)}) custom-call(bf16[128,3584]{1,0:T(8,128)(2,1)} %bitcast.11, bf16[448,4608]{1,0:T(8,128)(2,1)} %qkv_weight.1, bf16[448,3584]{1,0:T(8,128)(2,1)} %bitcast.10, s32[1,1]{1,0:T(1,128)} %bitcast.7.length_one, f32[1,1]{1,0:T(1,128)} %bitcast.8.pair_weight_one, s32[32]{0:T(128)} %partner_all.1, ...), custom_call_target="tpu_custom_call" | custom-call | tf_op jit(solution)/shard_map/pallas_call | solution.py:856
  122.0 0.5 fusion
  122.5 0.9 copy.16

commit v7 on v6

--- a/solution.py
+++ b/solution.py
@@ -96,8 +96,8 @@
 
 
 def out_pieces(out_cols):
-    big = (out_cols // 2 + HEAD_SIZE - 1) // HEAD_SIZE * HEAD_SIZE
-    return big, out_cols - big
+    small = HEAD_SIZE // 2
+    return out_cols - small, small
 
 
 def layer_kernel(
@@ -188,6 +188,7 @@
     is_end = (z == 0) | (z == line - 1)
     is_helper = (z == 1) | (z == line - 2)
     far = jnp.where((z == 0) | (z == 1), line - 1, 0)
+    near = jnp.where((z == 0) | (z == 1), line - 2, 1)
     end_to_helper = {"fsdp": jnp.where(z == 0, f + 2, f - 2)}
     helper_to_end = {"fsdp": jnp.where(z == 1, f - 2, f + 2)}
     has_up = z < line - 1
@@ -208,7 +209,8 @@
         def _():
             pl.semaphore_signal(barrier, inc=1, device_id=way_ids[way])
 
-    piece_sizes = (big, small, big // 2, big // 2)
+    edge = HEAD_SIZE
+    piece_sizes = (big, small, big - edge, edge)
     pieces = (((0, 1), (0, 1)), ((0, 1), (1, 2, 3)))
 
     def out_rows(side, piece, half):
@@ -216,8 +218,8 @@
         start = (
             side * small,
             (1 - side) * big,
-            (1 - side) * (big // 2) + side * small,
-            side * (small + big // 2),
+            (1 - side) * edge + side * small,
+            side * (out_cols - edge),
         )[piece]
         return start + half * size, size
 
@@ -360,6 +362,10 @@
         for ok, s, way, onward in sides(k, o):
             if m == 1:
                 onward = onward & (k < line - 2)
+            if m == 1 and piece == 1:
+                spot, target = (z - line + 2, 1) if way == UP else (z - 1, line - 2)
+                onward = onward & jnp.logical_not((spot == 0) & (s // 2 == target))
+                ok = ok & jnp.logical_not(is_end & (k == line - 2))
 
             @pl.when(ok)
             def _():
@@ -644,12 +650,12 @@
         project(place, big, 2 * small, 1)
 
     def cross_unit(piece):
-        inner = (1 - y) * (pair - big) + y * (big // 2)
-        outer = (1 - y) * (pair - big // 2)
+        inner = (1 - y) * (pair - big) + y * edge
+        outer = (1 - y) * (pair - edge)
 
         def body(place):
             arrived(1, 2 * place + 1 - y, piece, 1)
-            project(place, (inner, outer)[piece - 2], big // 2, 0)
+            project(place, (inner, outer)[piece - 2], piece_sizes[piece], 0)
 
         return body
 
@@ -669,7 +675,7 @@
 
         line_step(1, k, 1, 0)
 
-        @pl.when(mine)
+        @pl.when(mine & jnp.logical_not(is_end & (k == line - 2)))
         def _():
             at_sides(k, mid_unit)
 
@@ -713,6 +719,13 @@
                 (((1,), (1,)), ((), ())),
                 preferred_element_type=jnp.float32,
             )
+            middle = lax.dot_general(
+                attn_help[rows, :],
+                out_full[lanes_of(near * pair + big, 2 * small), :],
+                (((1,), (1,)), ((), ())),
+                preferred_element_type=jnp.float32,
+            )
+            result = jnp.concatenate([result, middle], axis=1)
             help_own[...] = result
             help_out[j] = result.astype(jnp.bfloat16)
             for way in range(3):
@@ -734,9 +747,26 @@
 
     @pl.when(is_end)
     def _():
-        at_sides(line - 2, finish_parts)
+        for way in range(3):
+            bytes_of(
+                part_in.at[way, near, :, pl.ds(0, pair - 2 * small)], part_recv.at[way, near]
+            ).wait()
         done_copy.wait_recv()
-        finish(far, help_done[...].astype(jnp.float32))
+
+        def near_cols(lanes):
+            total = own[near, :, lanes]
+            for way in range(3):
+                total += part_in[way, near, :, lanes].astype(jnp.float32)
+            return total
+
+        middle = help_done[:, pair:].astype(jnp.float32)
+        finish(
+            near,
+            jnp.concatenate(
+                [near_cols(slice(0, big)), middle, near_cols(slice(pair - big, pair))], axis=1
+            ),
+        )
+        finish(far, help_done[:, :pair].astype(jnp.float32))
 
     @pl.when(is_helper)
     def _():
@@ -783,10 +813,14 @@
                 if slices:
                     rows = pl.ds(0, slices * depth // 2)
                     bytes_of(qkv_full.at[rows], send_sem.at[way, 0]).wait()
-                    rows = pl.ds(0, out_slices * out_cols // 2)
+                    less = small * (spot == (line - 2, 1, spot * ends + (1 - ends) * line)[way])
+                    rows = pl.ds(0, out_slices * out_cols // 2 - less)
                     bytes_of(out_full.at[rows], send_sem.at[way, 1]).wait()
             for way in range(3):
-                bytes_of(part_in.at[0, pl.ds(0, line - ends)], part_send.at[way]).wait()
+                sums = part_in.at[0]
+                if ends:
+                    sums = part_out.at[0, :, pl.ds(0, ((line - 1) * pair - 2 * small) // groups)]
+                bytes_of(sums, part_send.at[way]).wait()
             if ends:
                 bytes_of(attn, attn_send.at[0]).wait()
 
@@ -815,15 +849,15 @@
 
 def layer_fits(shards, groups, tokens, qkv_weight, out_weight):
     return (
-        shards % 2 == 0
-        and shards >= 8
+        shards == 8
         and qkv_weight.shape[0] % 64 == 0
         and groups == 4
         and KEY_VALUE_HEADS % groups == 0
         and tokens.shape[1] == HEAD_SIZE
         and shards * groups <= HEAD_SIZE
         and out_weight.shape[1] % 64 == 0
-        and out_weight.shape[1] > HEAD_SIZE
+        and out_weight.shape[1] % HEAD_SIZE == HEAD_SIZE // 2
+        and out_weight.shape[1] > 2 * HEAD_SIZE
     )
 
 
@@ -876,11 +910,11 @@
             pltpu.VMEM((line, rows, pair), bf16),
             pltpu.VMEM((groups - 1, line, seq_rows, pair), bf16),
             pltpu.VMEM((rows, query_cols), bf16),
-            pltpu.VMEM((seq_rows, pair), f32),
-            pltpu.VMEM((groups, seq_rows, pair), bf16),
-            pltpu.VMEM((groups - 1, seq_rows, pair), bf16),
-            pltpu.VMEM((seq_rows, pair), bf16),
-            pltpu.VMEM((seq_rows, pair), bf16),
+            pltpu.VMEM((seq_rows, pair + HEAD_SIZE), f32),
+            pltpu.VMEM((groups, seq_rows, pair + HEAD_SIZE), bf16),
+            pltpu.VMEM((groups - 1, seq_rows, pair + HEAD_SIZE), bf16),
+            pltpu.VMEM((seq_rows, pair + HEAD_SIZE), bf16),
+            pltpu.VMEM((seq_rows, pair + HEAD_SIZE), bf16),
             pltpu.VMEM((2, 8, HEAD_SIZE), f32),
             pltpu.VMEM((query_cols * HEAD_SIZE // key_cols, HEAD_SIZE), bf16),
             pltpu.VMEM((query_cols * HEAD_SIZE // key_cols, HEAD_SIZE), f32),

time: 124 us -> 121 us (0.976)
  Pallas kernels: 120 us -> 117 us
    pallas_call x1, Pallas kernels: 120 us -> 117 us  [layer(): pl.pallas_call(functools.partial(layer_kernel, shards, groups), out_shape...]
where the time goes in v7:
time: 121 us
  Pallas kernels  117 us (97%)
  between operations  1.93 us (2%)
  local copies, waits for them, and re-layouts  1.44 us (1%)
    pallas_call x1, Pallas kernels, layer(): pl.pallas_call(functools.partial(layer_kernel, shards, groups), out_shape...  117 us

profile of v7, /device:TPU:0, one launch (start us, length us, event | category | flops | bytes accessed | tf_op | source)
XLA Modules:
  0.0 120.6 jit_solution(8595857966835664414)
XLA Ops:
  1.9 117.2 %shard_map.139 = (bf16[128,3584]{1,0:T(8,128)(2,1)S(1)}, f32[8,128]{1,0:T(8,128)S(1)}) custom-call(bf16[128,3584]{1,0:T(8,128)(2,1)} %bitcast.11, bf16[448,4608]{1,0:T(8,128)(2,1)} %qkv_weight.1, bf16[448,3584]{1,0:T(8,128)(2,1)} %bitcast.10, s32[1,1]{1,0:T(1,128)} %bitcast.7.length_one, f32[1,1]{1,0:T(1,128)} %bitcast.8.pair_weight_one, s32[32]{0:T(128)} %partner_all.1, ...), custom_call_target="tpu_custom_call" | custom-call | tf_op jit(solution)/shard_map/pallas_call | solution.py:890
  119.1 0.5 fusion
  119.7 0.9 copy.16

commit v8 on v7

--- a/solution.py
+++ b/solution.py
@@ -389,8 +389,8 @@
         return pltpu.make_async_remote_copy(
             src_ref=normed.at[pl.ds(source * seq_rows + start, size)],
             dst_ref=normed.at[pl.ds((1 + way) * seq_rows + start, size)],
-            send_sem=tok_send.at[way],
-            recv_sem=tok_recv.at[way, piece],
+            send_sem=tok_send.at[0],
+            recv_sem=tok_recv.at[min(3 * way + piece, 6)],
             device_id=target,
         )
 
@@ -458,8 +458,9 @@
     for k, o, j in steps[:-1]:
         line_step(0, k, o, j)
 
-    for way, piece in ((0, 1), (0, 2), (1, 0), (2, 0), (2, 1), (2, 2)):
+    for way, piece in ((0, 1), (0, 2), (1, 0)):
         tok_copy(way, piece).wait_recv()
+    bytes_of(normed.at[pl.ds(3 * seq_rows, seq_rows)], tok_recv.at[6]).wait()
     bytes_of(len_all.at[pl.ds(1, 3)], len_sem.at[1]).wait()
     for copy in (*late_loads, *small_loads):
         copy.wait()
@@ -527,7 +528,7 @@
         return pltpu.make_async_remote_copy(
             src_ref=part_out.at[place, pl.ds((1 + way) * seq_rows, seq_rows), cols],
             dst_ref=part_in.at[way, place, :, cols],
-            send_sem=part_send.at[way],
+            send_sem=part_send.at[0],
             recv_sem=part_recv.at[way, place],
             device_id=team_ids[way],
         )
@@ -691,7 +692,7 @@
             src_ref=help_out.at[1 + way],
             dst_ref=help_in.at[way],
             send_sem=help_send.at[0],
-            recv_sem=help_recv.at[way],
+            recv_sem=help_recv.at[0],
             device_id=team_ids[way],
         )
 
@@ -737,8 +738,7 @@
         def _(place):
             pl.when(place != far)(lambda: finish_parts(place))
 
-        for way in range(3):
-            help_part(way).wait_recv()
+        bytes_of(help_in, help_recv.at[0]).wait()
         total = help_own[...]
         for way in range(3):
             total += help_in[way].astype(jnp.float32)
@@ -795,8 +795,7 @@
     bytes_of(cross_qkv, cross_send.at[0]).wait()
     bytes_of(out_full.at[pl.ds(0, out_cols // 2)], cross_send.at[1]).wait()
     bytes_of(len_all.at[pl.ds(1, 3)], len_sem.at[0]).wait()
-    for way in range(3):
-        bytes_of(normed.at[pl.ds(0, seq_rows)], tok_send.at[way]).wait()
+    bytes_of(normed.at[pl.ds(0, 3 * seq_rows)], tok_send.at[0]).wait()
     for spot in range(line):
         ends = spot in (0, line - 1)
         up = 0 if spot == line - 1 else 2 * (spot + 1)
@@ -816,11 +815,11 @@
                     less = small * (spot == (line - 2, 1, spot * ends + (1 - ends) * line)[way])
                     rows = pl.ds(0, out_slices * out_cols // 2 - less)
                     bytes_of(out_full.at[rows], send_sem.at[way, 1]).wait()
-            for way in range(3):
-                sums = part_in.at[0]
-                if ends:
-                    sums = part_out.at[0, :, pl.ds(0, ((line - 1) * pair - 2 * small) // groups)]
-                bytes_of(sums, part_send.at[way]).wait()
+            sums = part_in
+            if ends:
+                cols = pl.ds(0, ((line - 1) * pair - 2 * small) // groups)
+                sums = part_out.at[pl.ds(0, 3), :, cols]
+            bytes_of(sums, part_send.at[0]).wait()
             if ends:
                 bytes_of(attn, attn_send.at[0]).wait()
 
@@ -935,15 +934,15 @@
             dma((shards, 3, 2)),
             dma((3, 2)),
             dma((2,)),
-            dma((3,)),
-            dma((3, 3)),
+            dma((1,)),
+            dma((7,)),
             dma((2,)),
-            dma((3,)),
+            dma((1,)),
             dma((3, line)),
             dma((1,)),
             dma((groups,)),
             dma((1,)),
-            dma((3,)),
+            dma((1,)),
             dma((2,)),
             dma((2,)),
         ],

time: 121 us -> 121 us (level)
  no operation moved by 1% of the time
where the time goes in v8:
time: 121 us
  Pallas kernels  117 us (97%)
  between operations  1.93 us (2%)
  local copies, waits for them, and re-layouts  1.44 us (1%)
    pallas_call x1, Pallas kernels, layer(): pl.pallas_call(functools.partial(layer_kernel, shards, groups), out_shape...  117 us

profile of v8, /device:TPU:0, one launch (start us, length us, event | category | flops | bytes accessed | tf_op | source)
XLA Modules:
  0.0 120.5 jit_solution(6015302479377603873)
XLA Ops:
  1.9 117.1 %shard_map.139 = (bf16[128,3584]{1,0:T(8,128)(2,1)S(1)}, f32[8,128]{1,0:T(8,128)S(1)}) custom-call(bf16[128,3584]{1,0:T(8,128)(2,1)} %bitcast.11, bf16[448,4608]{1,0:T(8,128)(2,1)} %qkv_weight.1, bf16[448,3584]{1,0:T(8,128)(2,1)} %bitcast.10, s32[1,1]{1,0:T(1,128)} %bitcast.7.length_one, f32[1,1]{1,0:T(1,128)} %bitcast.8.pair_weight_one, s32[32]{0:T(128)} %partner_all.1, ...), custom_call_target="tpu_custom_call" | custom-call | tf_op jit(solution)/shard_map/pallas_call | solution.py:889
  119.1 0.5 fusion
  119.6 0.9 copy.16
